TPU v7x, 256 devices: a whole 4x4x8 slice. The times are simulated.
256 devices in a mesh: row: 32 (over y, x, core), gz: 8 (over z).
Axes of the slice: x: 4, y: 4, z: 8, core: 2. Of those that a mesh axis runs over, the one named last changes fastest.
Arguments:
- velocity_x: bfloat16 [2, 32, 1024, 1024], P(None, None, 'row', 'gz'), may hold values from -6 to 6
- velocity_y: bfloat16 [2, 32, 1024, 1024], P(None, None, 'row', 'gz'), may hold values from -6 to 6
- velocity_z: bfloat16 [2, 32, 1024, 1024], P(None, None, 'row', 'gz'), may hold values from -6 to 6
- spacing: float32 [64], replicated, may hold values from 0.5 to 2
- level_index: int32 [1024], replicated, may hold values from 0 to 63
- plane_index: int32 [32], replicated, may hold values from 4 to 128
Outputs:
- pressure: float32 [2, 32, 1024, 1024], P(None, None, 'row', 'gz')
All inputs are finite; a program needn't handle non-finite values.
Results may differ from a plain program's by a relative error of at most 0.002.
The roundings to bfloat16 on the way count: a program that leaves them out, or rounds other values in their place, can miss the bound.
Values may be sent and summed in bfloat16 or wider, within the bound.
A program may use at most 64 MiB of HBM per device.

v0:
```python
import math

import jax
import jax.numpy as jnp
import numpy as np
from jax import lax
from jax.experimental import pallas as pl
from jax.experimental.pallas import tpu as pltpu
from jax.sharding import PartitionSpec as P

MESH = pl.DeviceIdType.MESH
f32 = jnp.float32
bf16 = jnp.bfloat16
full_turn = 2.0 * math.pi
wave_unit = 2.0 * math.pi / 2048.0
ROW = 32
GZ = 8
DEPTH = 128
RADIX = 8
HALF = DEPTH // 2
ROOT_HALF = math.sqrt(0.5)


def tables():
    idx = np.arange(128)
    angle = 2.0 * np.pi / 128.0 * ((idx[:, None] * idx[None, :]) % 128)
    c, s = np.cos(angle), np.sin(angle)
    w = np.block([[c, -s], [s, c]]).astype(np.float32)
    hi = w.astype(jnp.bfloat16)
    lo = (w - hi.astype(np.float32)).astype(jnp.bfloat16)
    weights = np.concatenate([hi, hi, lo], axis=0)
    twist = 2.0 * np.pi / 1024.0 * (np.arange(8)[:, None] * idx[None, :])
    twiddle = np.concatenate([np.cos(twist), np.sin(twist)], axis=0).astype(np.float32)
    return weights, twiddle


def butterfly(xr, xi):
    def add(p, q):
        return (p[0] + q[0], p[1] + q[1])

    def sub(p, q):
        return (p[0] - q[0], p[1] - q[1])

    def turn(p):
        return (p[1], -p[0])

    x = list(zip(xr, xi))
    a0, a1 = add(x[0], x[4]), sub(x[0], x[4])
    a2, a3 = add(x[2], x[6]), turn(sub(x[2], x[6]))
    b0, b1 = add(x[1], x[5]), sub(x[1], x[5])
    b2, b3 = add(x[3], x[7]), turn(sub(x[3], x[7]))
    e = [add(a0, a2), add(a1, a3), sub(a0, a2), sub(a1, a3)]
    o = [add(b0, b2), add(b1, b3), sub(b0, b2), sub(b1, b3)]
    o1 = ((o[1][0] + o[1][1]) * ROOT_HALF, (o[1][1] - o[1][0]) * ROOT_HALF)
    o2 = turn(o[2])
    o3 = ((o[3][1] - o[3][0]) * ROOT_HALF, -(o[3][0] + o[3][1]) * ROOT_HALF)
    odd = [o[0], o1, o2, o3]
    return [add(e[k], odd[k]) for k in range(4)] + [sub(e[k], odd[k]) for k in range(4)]


def twisted(re, im, tw_ref, c):
    if c == 0:
        return re, im
    cos = tw_ref[c : c + 1, :]
    sin = tw_ref[8 + c : 9 + c, :]
    return re * cos + im * sin, im * cos - re * sin


def put_split(y_ref, c, rows, re, im):
    re_hi = re.astype(bf16)
    im_hi = im.astype(bf16)
    y_ref[c, rows, 0:128] = re_hi
    y_ref[c, rows, 128:256] = im_hi
    y_ref[c, rows, 256:384] = (re - re_hi.astype(f32)).astype(bf16)
    y_ref[c, rows, 384:512] = (im - im_hi.astype(f32)).astype(bf16)


def kernel(
    u_hbm, v_hbm, w_hbm, spacing_ref, level_ref, plane_ref, weights_ref, tw_ref,
    out_ref,
    u_v, v_v, w_v, s_v, recv_u, recv_s, out_v, halo_out, halo_in, halo_cols, band, bmat,
    inv_s, fe_s, bc_s, vs_s, ws_s, vt_s, wt_s, yt_s, rhs, part, q_t, y_s, kx_s,
    sp_all, ex_all, sp_send, ex_send, red, edge,
    lsem, bar_send, bar_recv,
):
    me = lax.axis_index("row")
    g = lax.axis_index("gz")
    barrier = pltpu.get_barrier_semaphore()
    loads = [
        pltpu.make_async_copy(w_hbm, w_v, lsem.at[0]),
        pltpu.make_async_copy(u_hbm, u_v, lsem.at[1]),
        pltpu.make_async_copy(v_hbm, v_v, lsem.at[2]),
    ]
    for load in loads:
        load.start()

    def greet_row(d, carry):
        pl.semaphore_signal(
            barrier, inc=1, device_id={"row": lax.rem(me + d, ROW)}, device_id_type=MESH
        )
        return carry

    def greet_gz(d, carry):
        pl.semaphore_signal(
            barrier, inc=1, device_id={"gz": lax.rem(g + d, GZ)}, device_id_type=MESH
        )
        return carry

    lax.fori_loop(1, ROW, greet_row, 0)
    lax.fori_loop(1, GZ, greet_gz, 0)

    def row_send(src, dst, k, t):
        return pltpu.make_async_remote_copy(
            src, dst, bar_send.at[k], bar_recv.at[k], device_id={"row": t}, device_id_type=MESH
        )

    def gz_send(src, dst, k, t):
        return pltpu.make_async_remote_copy(
            src, dst, bar_send.at[k], bar_recv.at[k], device_id={"gz": t}, device_id_type=MESH
        )

    level = level_ref[...]
    width = jnp.zeros((GZ, DEPTH), f32)
    for n in range(64):
        width = jnp.where(level == n, spacing_ref[n], width)
    lane = lax.broadcasted_iota(jnp.int32, (GZ, DEPTH), 1)
    block = lax.broadcasted_iota(jnp.int32, (GZ, DEPTH), 0)
    shift_up = pltpu.roll(width, 1, 1)
    previous = jnp.where(lane == 0, pltpu.roll(shift_up, 1, 0), shift_up)
    shift_down = pltpu.roll(width, DEPTH - 1, 1)
    following = jnp.where(lane == DEPTH - 1, pltpu.roll(shift_down, GZ - 1, 0), shift_down)
    lower = 1.0 / (0.5 * (previous + width) * width)
    upper = 1.0 / (0.5 * (width + following) * width)
    lower = jnp.where((lane == 0) & (block == 0), 0.0, lower)
    upper = jnp.where((lane == DEPTH - 1) & (block == GZ - 1), 0.0, upper)
    band[0] = lower
    band[1] = upper
    band[2] = -(lower + upper)
    band[3] = 1.0 / width
    for n in range(3):
        row_n = jnp.broadcast_to(band[n, pl.ds(g, 1), :], (DEPTH, DEPTH))
        bmat[n] = row_n.T

    loads[0].wait()
    pick = (lax.broadcasted_iota(jnp.int32, (16, DEPTH), 1) == DEPTH - 1).astype(f32).astype(bf16)
    for n in range(2):
        column = lax.dot_general(
            pick,
            w_v[n].reshape(1024, DEPTH),
            (((1,), (1,)), ((), ())),
            preferred_element_type=f32,
        )
        halo_out[:, n * 1024 : (n + 1) * 1024] = column[0:1, :]
    loads[1].wait()
    loads[2].wait()
    pl.semaphore_wait(barrier, ROW - 1 + GZ - 1)

    above = lax.rem(g + 1, GZ)
    halo_copy = gz_send(halo_out, halo_in, 0, above)
    halo_copy.start()

    def send_u(d, carry):
        t = lax.rem(me + d, ROW)
        row_send(u_v.at[:, t], recv_u.at[:, me], 1, t).start()
        return carry

    lax.fori_loop(1, ROW, send_u, 0)
    recv_u[:, pl.ds(me, 1)] = u_v[:, pl.ds(me, 1)]

    halo_copy.wait()
    has_below = jnp.where(g > 0, 1.0, 0.0)
    first_lane = (lax.broadcasted_iota(jnp.int32, (8, DEPTH), 1) == 0).astype(f32)
    first_row = (lax.broadcasted_iota(jnp.int32, (8, DEPTH), 0) == 0).astype(f32)
    spot = (first_lane * first_row * has_below).astype(bf16)
    for n in range(2):
        wide = jnp.broadcast_to(halo_in[:, n * 1024 : (n + 1) * 1024], (8, 1024)).astype(bf16)
        halo_cols[n] = lax.dot_general(
            wide, spot, (((0,), (0,)), ((), ())), preferred_element_type=f32
        ).reshape(32, 32, DEPTH)
    inv_width = band[3, pl.ds(g, 1), :]
    lane32 = lax.broadcasted_iota(jnp.int32, (32, DEPTH), 1)

    def make_source(t):
        wave = plane_ref[t].astype(f32) * wave_unit
        slopes = []
        for n in range(2):
            upward = w_v[n, t].astype(f32)
            below = jnp.where(lane32 == 0, halo_cols[n, t], pltpu.roll(upward, 1, 1))
            slopes.append((upward - below) * inv_width)
        s_v[0, t] = (-wave * v_v[1, t].astype(f32) + slopes[0]).astype(bf16)
        s_v[1, t] = (wave * v_v[0, t].astype(f32) + slopes[1]).astype(bf16)

    def send_s(t):
        row_send(s_v.at[:, t], recv_s.at[:, me], 2, t).start()

    make_source(lax.rem(me + 1, ROW))

    def source_step(d, carry):
        make_source(lax.rem(me + d, ROW))
        send_s(lax.rem(me + d - 1, ROW))
        return carry

    lax.fori_loop(2, ROW, source_step, 0)
    make_source(me)
    send_s(lax.rem(me + ROW - 1, ROW))
    recv_s[:, pl.ds(me, 1)] = s_v[:, pl.ds(me, 1)]

    outer = lax.broadcasted_iota(jnp.int32, (RADIX, 128), 0)
    inner = lax.broadcasted_iota(jnp.int32, (RADIX, 128), 1)
    mode = 8 * inner + outer
    mode = jnp.where(mode >= 512, mode - 1024, mode)
    wave_x = mode.astype(f32) * (full_turn / 1024.0)
    own_wave = plane_ref[me].astype(f32) * wave_unit
    wave_sq = wave_x * wave_x + own_wave * own_wave
    kx_s[...] = wave_x

    def coef(n, z):
        return jnp.broadcast_to(bmat[n, pl.ds(z, 1), :], (RADIX, 128))

    def factor(j, carry):
        top, bottom, v_top, w_bottom = carry
        z = j
        lo, up = coef(0, z), coef(1, z)
        inv = 1.0 / ((coef(2, z) - wave_sq) - lo * top)
        fe = lo * inv
        top = up * inv
        inv_s[z] = inv
        fe_s[z] = fe
        bc_s[z] = top
        v_top = -fe * v_top
        vs_s[pl.ds(pl.multiple_of(z * 8, 8), 8), :] = v_top
        z = DEPTH - 1 - j
        lo, up = coef(0, z), coef(1, z)
        inv = 1.0 / ((coef(2, z) - wave_sq) - up * bottom)
        fe = up * inv
        bottom = lo * inv
        inv_s[z] = inv
        fe_s[z] = fe
        bc_s[z] = bottom
        w_bottom = -fe * w_bottom
        ws_s[pl.ds(pl.multiple_of(z * 8, 8), 8), :] = w_bottom
        return top, bottom, v_top, w_bottom

    zero = jnp.zeros((RADIX, 128), f32)
    one = jnp.ones((RADIX, 128), f32)
    top, bottom, v_top, w_bottom = lax.fori_loop(0, HALF, factor, (zero, zero, one, one))
    inv_det = 1.0 / (1.0 - top * bottom)

    def at(z):
        return pl.ds(pl.multiple_of(z * 8, 8), 8)

    v_lo = v_top * inv_det
    v_hi = -bottom * v_lo
    w_hi = w_bottom * inv_det
    w_lo = -top * w_hi
    vs_s[at(HALF - 1), :] = v_lo
    vs_s[at(HALF), :] = v_hi
    ws_s[at(HALF - 1), :] = w_lo
    ws_s[at(HALF), :] = w_hi

    def spread(j, carry):
        v_lo, v_hi, w_lo, w_hi = carry
        z = HALF - 1 - j
        bc = bc_s[z]
        v_lo = vs_s[at(z), :] - bc * v_lo
        w_lo = -bc * w_lo
        vs_s[at(z), :] = v_lo
        ws_s[at(z), :] = w_lo
        z = HALF + j
        bc = bc_s[z]
        v_hi = -bc * v_hi
        w_hi = ws_s[at(z), :] - bc * w_hi
        vs_s[at(z), :] = v_hi
        ws_s[at(z), :] = w_hi
        return v_lo, v_hi, w_lo, w_hi

    v_lo, v_hi, w_lo, w_hi = lax.fori_loop(1, HALF, spread, (v_lo, v_hi, w_lo, w_hi))
    sp_send[0] = v_lo
    sp_send[1] = v_hi
    sp_send[2] = w_lo
    sp_send[3] = w_hi
    sp_all[pl.ds(g, 1)] = sp_send[...][None]
    for c in range(RADIX):
        vt_s[c] = vs_s[pl.ds(c, DEPTH, stride=8), :]
        wt_s[c] = ws_s[pl.ds(c, DEPTH, stride=8), :]

    def send_sp(d, carry):
        t = lax.rem(g + d, GZ)
        gz_send(sp_send, sp_all.at[g], 3, t).start()
        return carry

    lax.fori_loop(1, GZ, send_sp, 0)

    def forward(recv, finish):
        def flip(a, carry):
            for n in range(2):
                q_t[n, a] = recv[n, pl.ds(4 * a, 4)].reshape(128, 128).T
            return carry

        lax.fori_loop(0, RADIX, flip, 0)

        def mix(i, carry):
            rows = pl.ds(pl.multiple_of(16 * i, 16), 16)
            xr = [q_t[0, a, rows, :].astype(f32) for a in range(RADIX)]
            xi = [q_t[1, a, rows, :].astype(f32) for a in range(RADIX)]
            for c, (re, im) in enumerate(butterfly(xr, xi)):
                re, im = twisted(re, im, tw_ref, c)
                put_split(y_s, c, rows, re, im)
            return carry

        lax.fori_loop(0, DEPTH // 16, mix, 0)
        for c in range(0, RADIX, 2):
            finish(c, product(c))

    def product(c):
        rows = y_s[c : c + 2].reshape(2 * DEPTH, 512)
        return jnp.dot(rows, weights_ref[0:512, :], preferred_element_type=f32) + jnp.dot(
            rows[:, 0:256], weights_ref[512:768, :], preferred_element_type=f32
        )

    def keep_along(c, acc):
        for n in range(2):
            kx = kx_s[c + n : c + n + 1, :]
            own = acc[n * DEPTH : (n + 1) * DEPTH]
            part[c + n, :, 0:128] = -kx * own[:, 128:256]
            part[c + n, :, 128:256] = kx * own[:, 0:128]

    def keep_rhs(c, acc):
        for n in range(2):
            total = acc[n * DEPTH : (n + 1) * DEPTH] + part[c + n]
            rhs[0, pl.ds(c + n, DEPTH, stride=8), :] = total[:, 0:128]
            rhs[1, pl.ds(c + n, DEPTH, stride=8), :] = total[:, 128:256]

    def row_wait(ref, k):
        row_send(ref.at[:, 0 : ROW - 1], ref.at[:, 0 : ROW - 1], k, me).wait_recv()

    row_wait(recv_u, 1)
    forward(recv_u, keep_along)

    gz_send(sp_all.at[0 : GZ - 1], sp_all.at[0 : GZ - 1], 3, g).wait_recv()
    beta = zero
    for b in range(GZ):
        v_first, v_last, w_first, w_last = (sp_all[b, n] for n in range(4))
        inv = 1.0 / (1.0 - v_first * beta)
        gamma = v_last * beta * inv
        red[0, b] = gamma
        red[1, b] = v_last + gamma * v_first
        red[2, b] = inv
        red[3, b] = inv * v_first
        red[4, b] = inv * w_first
        beta = w_last + gamma * w_first
        red[5, b] = beta

    row_wait(recv_s, 2)
    forward(recv_s, keep_rhs)

    def down(j, carry):
        out = []
        for z, pair in ((j, carry[0:2]), (DEPTH - 1 - j, carry[2:4])):
            inv, fe = inv_s[z], fe_s[z]
            for n in range(2):
                value = rhs[n, at(z), :] * inv - fe * pair[n]
                rhs[n, at(z), :] = value
                out.append(value)
        return tuple(out)

    low_re, low_im, high_re, high_im = lax.fori_loop(0, HALF, down, (zero,) * 4)
    bc_low, bc_high = bc_s[HALF - 1], bc_s[HALF]
    inv_det = 1.0 / (1.0 - bc_low * bc_high)
    low_re = (low_re - bc_low * high_re) * inv_det
    low_im = (low_im - bc_low * high_im) * inv_det
    high_re = high_re - bc_high * low_re
    high_im = high_im - bc_high * low_im
    rhs[0, at(HALF - 1), :] = low_re
    rhs[1, at(HALF - 1), :] = low_im
    rhs[0, at(HALF), :] = high_re
    rhs[1, at(HALF), :] = high_im

    def up_again(j, carry):
        out = []
        for z, pair in ((HALF - 1 - j, carry[0:2]), (HALF + j, carry[2:4])):
            bc = bc_s[z]
            for n in range(2):
                value = rhs[n, at(z), :] - bc * pair[n]
                rhs[n, at(z), :] = value
                out.append(value)
        return tuple(out)

    low_re, low_im, high_re, high_im = lax.fori_loop(
        1, HALF, up_again, (low_re, low_im, high_re, high_im)
    )
    ex_send[0] = low_re
    ex_send[1] = low_im
    ex_send[2] = high_re
    ex_send[3] = high_im
    ex_all[pl.ds(g, 1)] = ex_send[...][None]

    def send_ex(d, carry):
        t = lax.rem(g + d, GZ)
        gz_send(ex_send, ex_all.at[g], 4, t).start()
        return carry

    lax.fori_loop(1, GZ, send_ex, 0)
    for c in range(RADIX):
        for n in range(2):
            yt_s[n, c] = rhs[n, pl.ds(c, DEPTH, stride=8), :]
    gz_send(ex_all.at[0 : GZ - 1], ex_all.at[0 : GZ - 1], 4, g).wait_recv()

    for n in range(2):
        alpha = zero
        befores = []
        for b in range(GZ):
            befores.append(alpha)
            alpha = (
                ex_all[b, 2 + n] + red[0, b] * ex_all[b, n] + red[1, b] * alpha
            )
        first = zero
        edge[1, n, GZ - 1] = zero
        for b in range(GZ - 1, -1, -1):
            first = red[2, b] * ex_all[b, n] + red[3, b] * befores[b] + red[4, b] * first
            if b > 0:
                edge[1, n, b - 1] = first
                edge[0, n, b] = befores[b] + red[5, b - 1] * first
        edge[0, n, 0] = zero

    from_below = [edge[0, n, g] for n in range(2)]
    from_above = [edge[1, n, g] for n in range(2)]

    def correct(i, carry):
        rows = pl.ds(pl.multiple_of(16 * i, 16), 16)
        for c in range(RADIX):
            v_c, w_c = vt_s[c, rows, :], wt_s[c, rows, :]
            full = [
                yt_s[n, c, rows, :]
                + v_c * from_below[n][c : c + 1, :]
                + w_c * from_above[n][c : c + 1, :]
                for n in range(2)
            ]
            put_split(y_s, c, rows, full[1], full[0])
        return carry

    lax.fori_loop(0, DEPTH // 16, correct, 0)
    for c in range(0, RADIX, 2):
        part[c : c + 2] = product(c).reshape(2, DEPTH, 256)

    def unmix(i, carry):
        rows = pl.ds(pl.multiple_of(16 * i, 16), 16)
        turned = [
            twisted(part[c, rows, 0:128], part[c, rows, 128:256], tw_ref, c) for c in range(RADIX)
        ]
        mixed = butterfly([t[0] for t in turned], [t[1] for t in turned])
        for j, (first, second) in enumerate(mixed):
            q_t[0, j, rows, :] = second.astype(bf16)
            q_t[1, j, rows, :] = first.astype(bf16)
        return carry

    lax.fori_loop(0, DEPTH // 16, unmix, 0)

    start = me // 4

    def give(jj, carry):
        j = lax.rem(start + jj, RADIX)
        for n in range(2):
            out_v[n, pl.ds(4 * j, 4)] = q_t[n, j].T.reshape(4, 32, DEPTH)
        return carry

    def give_send(jj, carry):
        j = lax.rem(start + jj, RADIX)
        for n in range(4):
            t = 4 * j + n

            @pl.when(t != me)
            def _():
                row_send(out_v.at[:, t], out_ref.at[:, me], 5, t).start()

        return carry

    give(0, 0)

    def give_step(jj, carry):
        give(jj, carry)
        give_send(jj - 1, carry)
        return carry

    lax.fori_loop(1, RADIX, give_step, 0)
    own = pltpu.make_async_copy(out_v.at[:, me], out_ref.at[:, me], lsem.at[0])
    own.start()
    give_send(RADIX - 1, 0)
    own.wait()
    row_wait(out_ref, 5)
    for k, ref in ((1, u_v), (2, s_v), (5, out_v)):
        row_send(ref.at[:, 0 : ROW - 1], ref.at[:, 0 : ROW - 1], k, me).wait_send()
    for k, ref in ((3, sp_all), (4, ex_all)):
        gz_send(ref.at[0 : GZ - 1], ref.at[0 : GZ - 1], k, g).wait_send()


def on_device(velocity_x, velocity_y, velocity_z, spacing, level_index, plane_index):
    weights, twiddle = tables()
    block = (2, 32, 32, 128)
    line = (DEPTH, RADIX, 128)
    flat = (DEPTH * RADIX, 128)
    tile = (RADIX, DEPTH, 128)
    pressure = pl.pallas_call(
        kernel,
        out_shape=jax.ShapeDtypeStruct(block, bf16),
        in_specs=[
            pl.BlockSpec(memory_space=pl.ANY),
            pl.BlockSpec(memory_space=pl.ANY),
            pl.BlockSpec(memory_space=pl.ANY),
            pl.BlockSpec(memory_space=pltpu.SMEM),
            pl.BlockSpec(memory_space=pltpu.VMEM),
            pl.BlockSpec(memory_space=pltpu.SMEM),
            pl.BlockSpec(memory_space=pltpu.VMEM),
            pl.BlockSpec(memory_space=pltpu.VMEM),
        ],
        out_specs=pl.BlockSpec(memory_space=pl.ANY),
        scratch_shapes=[
            pltpu.VMEM(block, bf16),
            pltpu.VMEM(block, bf16),
            pltpu.VMEM(block, bf16),
            pltpu.VMEM(block, bf16),
            pltpu.VMEM(block, bf16),
            pltpu.VMEM(block, bf16),
            pltpu.VMEM(block, bf16),
            pltpu.VMEM((1, 2048), f32),
            pltpu.VMEM((1, 2048), f32),
            pltpu.VMEM(block, f32),
            pltpu.VMEM((4, 8, 128), f32),
            pltpu.VMEM((3, 128, 128), f32),
            pltpu.VMEM(line, f32),
            pltpu.VMEM(line, f32),
            pltpu.VMEM(line, f32),
            pltpu.VMEM(flat, f32),
            pltpu.VMEM(flat, f32),
            pltpu.VMEM(tile, f32),
            pltpu.VMEM(tile, f32),
            pltpu.VMEM((2,) + tile, f32),
            pltpu.VMEM((2,) + flat, f32),
            pltpu.VMEM((RADIX, DEPTH, 256), f32),
            pltpu.VMEM((2, RADIX, 128, 128), bf16),
            pltpu.VMEM((RADIX, DEPTH, 512), bf16),
            pltpu.VMEM((RADIX, 128), f32),
            pltpu.VMEM((GZ, 4, RADIX, 128), f32),
            pltpu.VMEM((GZ, 4, RADIX, 128), f32),
            pltpu.VMEM((4, RADIX, 128), f32),
            pltpu.VMEM((4, RADIX, 128), f32),
            pltpu.VMEM((6, GZ, RADIX, 128), f32),
            pltpu.VMEM((2, 2, GZ, RADIX, 128), f32),
            pltpu.SemaphoreType.DMA((3,)),
            pltpu.SemaphoreType.DMA((6,)),
            pltpu.SemaphoreType.DMA((6,)),
        ],
        compiler_params=pltpu.CompilerParams(
            collective_id=0, has_side_effects=True, vmem_limit_bytes=48 * 1024 * 1024
        ),
        name="poisson",
    )(
        velocity_x,
        velocity_y,
        velocity_z,
        spacing,
        level_index.reshape(8, 128),
        plane_index,
        jnp.asarray(weights),
        jnp.asarray(twiddle),
    )
    return pressure.astype(f32) * (1.0 / 1024.0)


def solution(mesh):
    placed = (
        P(None, None, "row", "gz"),
        P(None, None, "row", "gz"),
        P(None, None, "row", "gz"),
        P(),
        P(),
        P(),
    )
    return jax.shard_map(
        on_device, mesh=mesh, in_specs=placed, out_specs=P(None, None, "row", "gz"), check_vma=False
    )
```

profile of v0, /device:TPU:1, one launch (start us, length us, event | category | flops | bytes accessed | tf_op | source)
XLA Modules:
  0.0 51.6 jit_solution(16455713368204918016)
XLA Ops:
  0.0 0.0 copy-start.7
  0.0 0.0 copy-start.6
  0.0 0.7 %copy-done.7 = s32[32]{0:T(128)S(1)} copy-done((s32[32]{0:T(128)S(1)}, s32[32]{0:T(128)}, u32[]{:S(2)}) %copy-start.7) | copy-done | bytes 152
  0.7 0.0 copy-done.6
  0.7 0.0 copy-start
  0.7 1.0 %copy-done = bf16[2,32,32,128]{3,2,1,0:T(8,128)(2,1)S(1)} copy-done((bf16[2,32,32,128]{3,2,1,0:T(8,128)(2,1)S(1)}, bf16[2,32,32,128]{3,2,1,0:T(8,128)(2,1)}, u32[]{:S(2)}) %copy-start) | copy-done | bytes 524312
  1.7 0.0 copy-start.1
  1.7 1.0 %copy-done.1 = bf16[2,32,32,128]{3,2,1,0:T(8,128)(2,1)S(1)} copy-done((bf16[2,32,32,128]{3,2,1,0:T(8,128)(2,1)S(1)}, bf16[2,32,32,128]{3,2,1,0:T(8,128)(2,1)}, u32[]{:S(2)}) %copy-start.1) | copy-done | bytes 524312
  2.8 0.0 copy-start.2
  2.8 1.0 %copy-done.2 = bf16[2,32,32,128]{3,2,1,0:T(8,128)(2,1)S(1)} copy-done((bf16[2,32,32,128]{3,2,1,0:T(8,128)(2,1)S(1)}, bf16[2,32,32,128]{3,2,1,0:T(8,128)(2,1)}, u32[]{:S(2)}) %copy-start.2) | copy-done | bytes 524312
  3.8 0.0 copy-start.3
  3.8 1.0 %copy-done.3 = bf16[768,256]{1,0:T(8,128)(2,1)S(1)} copy-done((bf16[768,256]{1,0:T(8,128)(2,1)S(1)}, bf16[768,256]{1,0:T(8,128)(2,1)}, u32[]{:S(2)}) %copy-start.3) | copy-done | bytes 393240
  4.8 0.0 copy-start.4
  4.8 0.7 %copy-done.4 = f32[16,128]{1,0:T(8,128)S(1)} copy-done((f32[16,128]{1,0:T(8,128)S(1)}, f32[16,128]{1,0:T(8,128)}, u32[]{:S(2)}) %copy-start.4) | copy-done | bytes 8216
  5.5 0.0 copy-start.5
  5.5 0.7 %copy-done.5 = s32[1024]{0:T(1024)S(1)} copy-done((s32[1024]{0:T(1024)S(1)}, s32[1024]{0:T(1024)}, u32[]{:S(2)}) %copy-start.5) | copy-done | bytes 4120
  6.2 44.3 %poisson.1 = bf16[2,32,32,128]{3,2,1,0:T(8,128)(2,1)S(1)} custom-call(bf16[2,32,32,128]{3,2,1,0:T(8,128)(2,1)S(1)} %copy-done, bf16[2,32,32,128]{3,2,1,0:T(8,128)(2,1)S(1)} %copy-done.1, bf16[2,32,32,128]{3,2,1,0:T(8,128)(2,1)S(1)} %copy-done.2, f32[64]{0:T(128)S(1)} %copy-done.6, s32[8,128]{1,0:T(8,128)S(1)} %bitcast.1, s32[32]{0:T(128)S(1)} %copy-done.7, ...), custom_call_target="tpu_custom_call" | custom-call | tf_op jit(solution)/shard_map/poisson/pallas_call | solution.py:503
  50.5 1.1 %convert_multiply_fusion = f32[2,32,32,128]{3,2,1,0:T(8,128)} fusion(bf16[2,32,32,128]{3,2,1,0:T(8,128)(2,1)S(1)} %poisson.1), kind=kLoop, calls=%fused_computation | loop fusion | flops 524288 | bytes 1572864 | tf_op jit(solution)/shard_map/mul | solution.py:567
Async XLA Ops:
  0.0 0.7 %copy-start.7 = (s32[32]{0:T(128)S(1)}, s32[32]{0:T(128)}, u32[]{:S(2)}) copy-start(s32[32]{0:T(128)} %plane_ref.1) | copy-start | bytes 388
  0.0 0.7 %copy-start.6 = (f32[64]{0:T(128)S(1)}, f32[64]{0:T(128)}, u32[]{:S(2)}) copy-start(f32[64]{0:T(128)} %spacing_ref.1) | copy-start | bytes 772
  0.7 1.0 %copy-start = (bf16[2,32,32,128]{3,2,1,0:T(8,128)(2,1)S(1)}, bf16[2,32,32,128]{3,2,1,0:T(8,128)(2,1)}, u32[]{:S(2)}) copy-start(bf16[2,32,32,128]{3,2,1,0:T(8,128)(2,1)} %u_hbm.1) | copy-start | bytes 1572868
  1.7 1.0 %copy-start.1 = (bf16[2,32,32,128]{3,2,1,0:T(8,128)(2,1)S(1)}, bf16[2,32,32,128]{3,2,1,0:T(8,128)(2,1)}, u32[]{:S(2)}) copy-start(bf16[2,32,32,128]{3,2,1,0:T(8,128)(2,1)} %v_hbm.1) | copy-start | bytes 1572868
  2.8 1.0 %copy-start.2 = (bf16[2,32,32,128]{3,2,1,0:T(8,128)(2,1)S(1)}, bf16[2,32,32,128]{3,2,1,0:T(8,128)(2,1)}, u32[]{:S(2)}) copy-start(bf16[2,32,32,128]{3,2,1,0:T(8,128)(2,1)} %w_hbm.1) | copy-start | bytes 1572868
  3.8 1.0 %copy-start.3 = (bf16[768,256]{1,0:T(8,128)(2,1)S(1)}, bf16[768,256]{1,0:T(8,128)(2,1)}, u32[]{:S(2)}) copy-start(bf16[768,256]{1,0:T(8,128)(2,1)} %constant.6.clone.weights_ref) | copy-start | bytes 1179652
  4.8 0.7 %copy-start.4 = (f32[16,128]{1,0:T(8,128)S(1)}, f32[16,128]{1,0:T(8,128)}, u32[]{:S(2)}) copy-start(f32[16,128]{1,0:T(8,128)} %constant.7.clone.tw_ref) | copy-start | bytes 24580
  5.5 0.7 %copy-start.5 = (s32[1024]{0:T(1024)S(1)}, s32[1024]{0:T(1024)}, u32[]{:S(2)}) copy-start(s32[1024]{0:T(1024)} %param.12) | copy-start | bytes 12292
where the time goes:
time: 52 us; the launch traced here: 51.6 us
  Pallas kernels  44.3 us (85%)
  local copies, waits for them, and re-layouts  6.17 us (12%)
  other arithmetic  1.11 us (2%)
    pallas_call x1, Pallas kernels, on_device(): pl.pallas_call(kernel, out_shape=jax.ShapeDtypeStruct(block, bf16), in_sp...  44.3 us
    unnamed x16, local copies, waits for them, and re-layouts  6.17 us
    mul x1, other arithmetic, on_device(): return pressure.astype(f32) * (1.0 / 1024.0)  1.11 us

commit v1 on v0

--- a/solution.py
+++ b/solution.py
@@ -76,8 +76,9 @@
 
 
 def kernel(
-    u_hbm, v_hbm, w_hbm, spacing_ref, level_ref, plane_ref, weights_ref, tw_ref,
+    u_hbm, v_hbm, w_hbm, spacing_hbm, level_hbm, plane_hbm, weights_hbm, tw_hbm,
     out_ref,
+    spacing_ref, level_ref, plane_ref, weights_ref, tw_ref,
     u_v, v_v, w_v, s_v, recv_u, recv_s, out_v, halo_out, halo_in, halo_cols, band, bmat,
     inv_s, fe_s, bc_s, vs_s, ws_s, vt_s, wt_s, yt_s, rhs, part, q_t, y_s, kx_s,
     sp_all, ex_all, sp_send, ex_send, red, edge,
@@ -90,6 +91,11 @@
         pltpu.make_async_copy(w_hbm, w_v, lsem.at[0]),
         pltpu.make_async_copy(u_hbm, u_v, lsem.at[1]),
         pltpu.make_async_copy(v_hbm, v_v, lsem.at[2]),
+        pltpu.make_async_copy(level_hbm, level_ref, lsem.at[3]),
+        pltpu.make_async_copy(spacing_hbm, spacing_ref, lsem.at[4]),
+        pltpu.make_async_copy(plane_hbm, plane_ref, lsem.at[5]),
+        pltpu.make_async_copy(tw_hbm, tw_ref, lsem.at[6]),
+        pltpu.make_async_copy(weights_hbm, weights_ref, lsem.at[7]),
     ]
     for load in loads:
         load.start()
@@ -118,6 +124,9 @@
         return pltpu.make_async_remote_copy(
             src, dst, bar_send.at[k], bar_recv.at[k], device_id={"gz": t}, device_id_type=MESH
         )
+
+    for load in loads[3:]:
+        load.wait()
 
     level = level_ref[...]
     width = jnp.zeros((GZ, DEPTH), f32)
@@ -504,17 +513,16 @@
         kernel,
         out_shape=jax.ShapeDtypeStruct(block, bf16),
         in_specs=[
-            pl.BlockSpec(memory_space=pl.ANY),
-            pl.BlockSpec(memory_space=pl.ANY),
-            pl.BlockSpec(memory_space=pl.ANY),
-            pl.BlockSpec(memory_space=pltpu.SMEM),
-            pl.BlockSpec(memory_space=pltpu.VMEM),
-            pl.BlockSpec(memory_space=pltpu.SMEM),
-            pl.BlockSpec(memory_space=pltpu.VMEM),
-            pl.BlockSpec(memory_space=pltpu.VMEM),
-        ],
-        out_specs=pl.BlockSpec(memory_space=pl.ANY),
+            pl.BlockSpec(memory_space=pltpu.HBM),
+        ]
+        * 8,
+        out_specs=pl.BlockSpec(memory_space=pltpu.HBM),
         scratch_shapes=[
+            pltpu.SMEM((64,), f32),
+            pltpu.VMEM((8, 128), jnp.int32),
+            pltpu.SMEM((32,), jnp.int32),
+            pltpu.VMEM((768, 256), bf16),
+            pltpu.VMEM((16, 128), f32),
             pltpu.VMEM(block, bf16),
             pltpu.VMEM(block, bf16),
             pltpu.VMEM(block, bf16),
@@ -546,12 +554,12 @@
             pltpu.VMEM((4, RADIX, 128), f32),
             pltpu.VMEM((6, GZ, RADIX, 128), f32),
             pltpu.VMEM((2, 2, GZ, RADIX, 128), f32),
-            pltpu.SemaphoreType.DMA((3,)),
+            pltpu.SemaphoreType.DMA((8,)),
             pltpu.SemaphoreType.DMA((6,)),
             pltpu.SemaphoreType.DMA((6,)),
         ],
         compiler_params=pltpu.CompilerParams(
-            collective_id=0, has_side_effects=True, vmem_limit_bytes=48 * 1024 * 1024
+            collective_id=0, has_side_effects=True, vmem_limit_bytes=67043328
         ),
         name="poisson",
     )(

time: 52 us -> 46.1 us (0.89)
  local copies, waits for them, and re-layouts: 6.17 us -> 0 us
  other arithmetic: 1.11 us -> 2.15 us
    unnamed x16 -> x0, local copies, waits for them, and re-layouts: 6.17 us -> none
    mul x1, other arithmetic: 1.11 us -> 2.15 us  [on_device(): return pressure.astype(f32) * (1.0 / 1024.0)]
    pallas_call x1, Pallas kernels: 44.3 us -> 43.8 us  [on_device(): pl.pallas_call(kernel, out_shape=jax.ShapeDtypeStruct(block, bf16), in_sp...]
where the time goes in v1:
time: 46.1 us; the launch traced here: 45.9 us
  Pallas kernels  43.8 us (95%)
  other arithmetic  2.15 us (5%)
    pallas_call x1, Pallas kernels, on_device(): pl.pallas_call(kernel, out_shape=jax.ShapeDtypeStruct(block, bf16), in_sp...  43.8 us
    mul x1, other arithmetic, on_device(): return pressure.astype(f32) * (1.0 / 1024.0)  2.15 us

profile of v1, /device:TPU:1, one launch (start us, length us, event | category | flops | bytes accessed | tf_op | source)
XLA Modules:
  0.0 45.9 jit_solution(16297970286551281045)
XLA Ops:
  0.0 43.8 %poisson.1 = bf16[2,32,32,128]{3,2,1,0:T(8,128)(2,1)} custom-call(bf16[2,32,32,128]{3,2,1,0:T(8,128)(2,1)} %u_hbm.1, bf16[2,32,32,128]{3,2,1,0:T(8,128)(2,1)} %v_hbm.1, bf16[2,32,32,128]{3,2,1,0:T(8,128)(2,1)} %w_hbm.1, f32[64]{0:T(128)} %spacing_hbm.1, s32[8,128]{1,0:T(8,128)} %bitcast.1, s32[32]{0:T(128)} %plane_hbm.1, ...), custom_call_target="tpu_custom_call" | custom-call | tf_op jit(solution)/shard_map/poisson/pallas_call | solution.py:512
  43.8 2.2 %convert_multiply_fusion = f32[2,32,32,128]{3,2,1,0:T(8,128)} fusion(bf16[2,32,32,128]{3,2,1,0:T(8,128)(2,1)} %poisson.1), kind=kLoop, calls=%fused_computation | loop fusion | flops 524288 | bytes 1572864 | tf_op jit(solution)/shard_map/mul | solution.py:575

commit v2 on v1

--- a/solution.py
+++ b/solution.py
@@ -75,14 +75,18 @@
     y_ref[c, rows, 384:512] = (im - im_hi.astype(f32)).astype(bf16)
 
 
+def far_first(i):
+    return lax.rem(2 + i + (i // 2) * (1 + 2 * lax.rem(i, 2)), 4)
+
+
 def kernel(
-    u_hbm, v_hbm, w_hbm, spacing_hbm, level_hbm, plane_hbm, weights_hbm, tw_hbm,
+    u_hbm, v_hbm, w_hbm, spacing_hbm, level_hbm, plane_hbm, weights_hbm, weights_t_hbm, tw_hbm,
     out_ref,
-    spacing_ref, level_ref, plane_ref, weights_ref, tw_ref,
+    spacing_ref, level_ref, plane_ref, weights_ref, weights_t, tw_ref,
     u_v, v_v, w_v, s_v, recv_u, recv_s, out_v, halo_out, halo_in, halo_cols, band, bmat,
-    inv_s, fe_s, bc_s, vs_s, ws_s, vt_s, wt_s, yt_s, rhs, part, q_t, y_s, kx_s,
+    inv_s, fe_s, bc_s, vs_s, ws_s, vt_s, wt_s, yt_s, rhs, part, part_t, tc_s, ts_s, q_t, y_s, kx_s,
     sp_all, ex_all, sp_send, ex_send, red, edge,
-    lsem, bar_send, bar_recv,
+    lsem, bar_send, bar_recv, s_recv,
 ):
     me = lax.axis_index("row")
     g = lax.axis_index("gz")
@@ -96,6 +100,7 @@
         pltpu.make_async_copy(plane_hbm, plane_ref, lsem.at[5]),
         pltpu.make_async_copy(tw_hbm, tw_ref, lsem.at[6]),
         pltpu.make_async_copy(weights_hbm, weights_ref, lsem.at[7]),
+        pltpu.make_async_copy(weights_t_hbm, weights_t, lsem.at[8]),
     ]
     for load in loads:
         load.start()
@@ -127,6 +132,14 @@
 
     for load in loads[3:]:
         load.wait()
+
+    my_y, my_x, my_core = me // 8, lax.rem(me // 2, 4), lax.rem(me, 2)
+
+    def partner(i):
+        y = lax.rem(my_y + far_first(i // 8), 4)
+        x = lax.rem(my_x + far_first(lax.rem(i // 2, 4)), 4)
+        core = lax.rem(my_core + 1 + lax.rem(i, 2), 2)
+        return (y * 4 + x) * 2 + core
 
     level = level_ref[...]
     width = jnp.zeros((GZ, DEPTH), f32)
@@ -168,12 +181,12 @@
     halo_copy = gz_send(halo_out, halo_in, 0, above)
     halo_copy.start()
 
-    def send_u(d, carry):
-        t = lax.rem(me + d, ROW)
+    def send_u(i, carry):
+        t = partner(i)
         row_send(u_v.at[:, t], recv_u.at[:, me], 1, t).start()
         return carry
 
-    lax.fori_loop(1, ROW, send_u, 0)
+    lax.fori_loop(0, ROW - 1, send_u, 0)
     recv_u[:, pl.ds(me, 1)] = u_v[:, pl.ds(me, 1)]
 
     halo_copy.wait()
@@ -200,18 +213,25 @@
         s_v[1, t] = (wave * v_v[0, t].astype(f32) + slopes[1]).astype(bf16)
 
     def send_s(t):
-        row_send(s_v.at[:, t], recv_s.at[:, me], 2, t).start()
-
-    make_source(lax.rem(me + 1, ROW))
-
-    def source_step(d, carry):
-        make_source(lax.rem(me + d, ROW))
-        send_s(lax.rem(me + d - 1, ROW))
-        return carry
-
-    lax.fori_loop(2, ROW, source_step, 0)
+        pltpu.make_async_remote_copy(
+            s_v.at[:, t],
+            recv_s.at[:, me],
+            bar_send.at[2],
+            s_recv.at[me // 4],
+            device_id={"row": t},
+            device_id_type=MESH,
+        ).start()
+
+    make_source(partner(0))
+
+    def source_step(i, carry):
+        make_source(partner(i))
+        send_s(partner(i - 1))
+        return carry
+
+    lax.fori_loop(1, ROW - 1, source_step, 0)
     make_source(me)
-    send_s(lax.rem(me + ROW - 1, ROW))
+    send_s(partner(ROW - 2))
     recv_s[:, pl.ds(me, 1)] = s_v[:, pl.ds(me, 1)]
 
     outer = lax.broadcasted_iota(jnp.int32, (RADIX, 128), 0)
@@ -300,13 +320,18 @@
 
     lax.fori_loop(1, GZ, send_sp, 0)
 
-    def forward(recv, finish):
-        def flip(a, carry):
+    def forward(recv, ready, finish):
+        def flip(i, carry):
+            y = lax.rem(my_y + 4 - far_first(i), 4)
             for n in range(2):
-                q_t[n, a] = recv[n, pl.ds(4 * a, 4)].reshape(128, 128).T
+                ready(2 * y + n)
+            for n in range(2):
+                for h in range(2):
+                    a = 2 * y + h
+                    q_t[n, a] = recv[n, pl.ds(4 * a, 4)].reshape(128, 128).T
             return carry
 
-        lax.fori_loop(0, RADIX, flip, 0)
+        lax.fori_loop(0, 4, flip, 0)
 
         def mix(i, carry):
             rows = pl.ds(pl.multiple_of(16 * i, 16), 16)
@@ -343,8 +368,14 @@
     def row_wait(ref, k):
         row_send(ref.at[:, 0 : ROW - 1], ref.at[:, 0 : ROW - 1], k, me).wait_recv()
 
+    def turn_table(c, carry):
+        tc_s[c] = jnp.broadcast_to(tw_ref[pl.ds(c, 1), :], (128, 128)).T
+        ts_s[c] = jnp.broadcast_to(tw_ref[pl.ds(8 + c, 1), :], (128, 128)).T
+        return carry
+
+    lax.fori_loop(1, RADIX, turn_table, 0)
     row_wait(recv_u, 1)
-    forward(recv_u, keep_along)
+    forward(recv_u, lambda a: None, keep_along)
 
     gz_send(sp_all.at[0 : GZ - 1], sp_all.at[0 : GZ - 1], 3, g).wait_recv()
     beta = zero
@@ -360,20 +391,37 @@
         beta = w_last + gamma * w_first
         red[5, b] = beta
 
-    row_wait(recv_s, 2)
-    forward(recv_s, keep_rhs)
-
-    def down(j, carry):
-        out = []
-        for z, pair in ((j, carry[0:2]), (DEPTH - 1 - j, carry[2:4])):
-            inv, fe = inv_s[z], fe_s[z]
-            for n in range(2):
-                value = rhs[n, at(z), :] * inv - fe * pair[n]
-                rhs[n, at(z), :] = value
-                out.append(value)
-        return tuple(out)
-
-    low_re, low_im, high_re, high_im = lax.fori_loop(0, HALF, down, (zero,) * 4)
+    def s_ready(a):
+        def wait_for(count):
+            view = recv_s.at[:, 0:count]
+            pltpu.make_async_remote_copy(
+                view, view, bar_send.at[2], s_recv.at[a], device_id={"row": me}, device_id_type=MESH
+            ).wait_recv()
+
+        @pl.when(a == me // 4)
+        def _():
+            wait_for(3)
+
+        @pl.when(a != me // 4)
+        def _():
+            wait_for(4)
+
+    forward(recv_s, s_ready, keep_rhs)
+
+    def down(i, carry):
+        for h in range(8):
+            j = 8 * i + h
+            out = []
+            for z, pair in ((j, carry[0:2]), (DEPTH - 1 - j, carry[2:4])):
+                inv, fe = inv_s[z], fe_s[z]
+                for n in range(2):
+                    value = rhs[n, at(z), :] * inv - fe * pair[n]
+                    rhs[n, at(z), :] = value
+                    out.append(value)
+            carry = tuple(out)
+        return carry
+
+    low_re, low_im, high_re, high_im = lax.fori_loop(0, HALF // 8, down, (zero,) * 4)
     bc_low, bc_high = bc_s[HALF - 1], bc_s[HALF]
     inv_det = 1.0 / (1.0 - bc_low * bc_high)
     low_re = (low_re - bc_low * high_re) * inv_det
@@ -385,18 +433,21 @@
     rhs[0, at(HALF), :] = high_re
     rhs[1, at(HALF), :] = high_im
 
-    def up_again(j, carry):
-        out = []
-        for z, pair in ((HALF - 1 - j, carry[0:2]), (HALF + j, carry[2:4])):
-            bc = bc_s[z]
-            for n in range(2):
-                value = rhs[n, at(z), :] - bc * pair[n]
-                rhs[n, at(z), :] = value
-                out.append(value)
-        return tuple(out)
+    def up_again(i, carry):
+        for h in range(7):
+            j = 7 * i + h + 1
+            out = []
+            for z, pair in ((HALF - 1 - j, carry[0:2]), (HALF + j, carry[2:4])):
+                bc = bc_s[z]
+                for n in range(2):
+                    value = rhs[n, at(z), :] - bc * pair[n]
+                    rhs[n, at(z), :] = value
+                    out.append(value)
+            carry = tuple(out)
+        return carry
 
     low_re, low_im, high_re, high_im = lax.fori_loop(
-        1, HALF, up_again, (low_re, low_im, high_re, high_im)
+        0, (HALF - 1) // 7, up_again, (low_re, low_im, high_re, high_im)
     )
     ex_send[0] = low_re
     ex_send[1] = low_im
@@ -404,12 +455,8 @@
     ex_send[3] = high_im
     ex_all[pl.ds(g, 1)] = ex_send[...][None]
 
-    def send_ex(d, carry):
-        t = lax.rem(g + d, GZ)
-        gz_send(ex_send, ex_all.at[g], 4, t).start()
-        return carry
-
-    lax.fori_loop(1, GZ, send_ex, 0)
+    for d in (4, 3, 5, 2, 6, 1, 7):
+        gz_send(ex_send, ex_all.at[g], 4, lax.rem(g + d, GZ)).start()
     for c in range(RADIX):
         for n in range(2):
             yt_s[n, c] = rhs[n, pl.ds(c, DEPTH, stride=8), :]
@@ -450,33 +497,37 @@
 
     lax.fori_loop(0, DEPTH // 16, correct, 0)
     for c in range(0, RADIX, 2):
-        part[c : c + 2] = product(c).reshape(2, DEPTH, 256)
-
-    def unmix(i, carry):
-        rows = pl.ds(pl.multiple_of(16 * i, 16), 16)
-        turned = [
-            twisted(part[c, rows, 0:128], part[c, rows, 128:256], tw_ref, c) for c in range(RADIX)
-        ]
-        mixed = butterfly([t[0] for t in turned], [t[1] for t in turned])
-        for j, (first, second) in enumerate(mixed):
-            q_t[0, j, rows, :] = second.astype(bf16)
-            q_t[1, j, rows, :] = first.astype(bf16)
-        return carry
-
-    lax.fori_loop(0, DEPTH // 16, unmix, 0)
-
-    start = me // 4
-
-    def give(jj, carry):
-        j = lax.rem(start + jj, RADIX)
+        rows = y_s[c : c + 2].reshape(2 * DEPTH, 512)
+        across = (((1,), (1,)), ((), ()))
+        acc = lax.dot_general(
+            weights_t[:, 0:512], rows, across, preferred_element_type=f32
+        ) + lax.dot_general(
+            weights_t[:, 512:768], rows[:, 0:256], across, preferred_element_type=f32
+        )
         for n in range(2):
-            out_v[n, pl.ds(4 * j, 4)] = q_t[n, j].T.reshape(4, 32, DEPTH)
-        return carry
-
-    def give_send(jj, carry):
-        j = lax.rem(start + jj, RADIX)
-        for n in range(4):
-            t = 4 * j + n
+            for h in range(2):
+                part_t[n, c + h] = acc[n * 128 : (n + 1) * 128, h * DEPTH : (h + 1) * DEPTH]
+
+    def unmix(q, carry):
+        for h in range(2):
+            rows = pl.ds(pl.multiple_of(32 * q + 16 * h, 16), 16)
+            turned = []
+            for c in range(RADIX):
+                re, im = part_t[0, c, rows, :], part_t[1, c, rows, :]
+                if c > 0:
+                    cos, sin = tc_s[c, rows, :], ts_s[c, rows, :]
+                    re, im = re * cos + im * sin, im * cos - re * sin
+                turned.append((re, im))
+            mixed = butterfly([t[0] for t in turned], [t[1] for t in turned])
+            for j, (first, second) in enumerate(mixed):
+                out_v[0, 4 * j + q, 16 * h : 16 * h + 16, :] = second.astype(bf16)
+                out_v[1, 4 * j + q, 16 * h : 16 * h + 16, :] = first.astype(bf16)
+        return carry
+
+    def give(q, carry):
+        for i in range(RADIX):
+            y = lax.rem(my_y + (2, 3, 1, 0)[i // 2], 4)
+            t = 8 * y + 4 * (i % 2) + q
 
             @pl.when(t != me)
             def _():
@@ -484,17 +535,17 @@
 
         return carry
 
-    give(0, 0)
-
-    def give_step(jj, carry):
-        give(jj, carry)
-        give_send(jj - 1, carry)
-        return carry
-
-    lax.fori_loop(1, RADIX, give_step, 0)
+    unmix(0, 0)
+
+    def unmix_step(q, carry):
+        unmix(q, carry)
+        give(q - 1, carry)
+        return carry
+
+    lax.fori_loop(1, 4, unmix_step, 0)
     own = pltpu.make_async_copy(out_v.at[:, me], out_ref.at[:, me], lsem.at[0])
     own.start()
-    give_send(RADIX - 1, 0)
+    give(3, 0)
     own.wait()
     row_wait(out_ref, 5)
     for k, ref in ((1, u_v), (2, s_v), (5, out_v)):
@@ -515,13 +566,14 @@
         in_specs=[
             pl.BlockSpec(memory_space=pltpu.HBM),
         ]
-        * 8,
+        * 9,
         out_specs=pl.BlockSpec(memory_space=pltpu.HBM),
         scratch_shapes=[
             pltpu.SMEM((64,), f32),
             pltpu.VMEM((8, 128), jnp.int32),
             pltpu.SMEM((32,), jnp.int32),
             pltpu.VMEM((768, 256), bf16),
+            pltpu.VMEM((256, 768), bf16),
             pltpu.VMEM((16, 128), f32),
             pltpu.VMEM(block, bf16),
             pltpu.VMEM(block, bf16),
@@ -545,6 +597,9 @@
             pltpu.VMEM((2,) + tile, f32),
             pltpu.VMEM((2,) + flat, f32),
             pltpu.VMEM((RADIX, DEPTH, 256), f32),
+            pltpu.VMEM((2,) + tile, f32),
+            pltpu.VMEM(tile, f32),
+            pltpu.VMEM(tile, f32),
             pltpu.VMEM((2, RADIX, 128, 128), bf16),
             pltpu.VMEM((RADIX, DEPTH, 512), bf16),
             pltpu.VMEM((RADIX, 128), f32),
@@ -554,9 +609,10 @@
             pltpu.VMEM((4, RADIX, 128), f32),
             pltpu.VMEM((6, GZ, RADIX, 128), f32),
             pltpu.VMEM((2, 2, GZ, RADIX, 128), f32),
-            pltpu.SemaphoreType.DMA((8,)),
+            pltpu.SemaphoreType.DMA((9,)),
             pltpu.SemaphoreType.DMA((6,)),
             pltpu.SemaphoreType.DMA((6,)),
+            pltpu.SemaphoreType.DMA((8,)),
         ],
         compiler_params=pltpu.CompilerParams(
             collective_id=0, has_side_effects=True, vmem_limit_bytes=67043328
@@ -570,6 +626,7 @@
         level_index.reshape(8, 128),
         plane_index,
         jnp.asarray(weights),
+        jnp.asarray(weights.T),
         jnp.asarray(twiddle),
     )
     return pressure.astype(f32) * (1.0 / 1024.0)

time: 46.1 us -> 43.3 us (0.939)
  Pallas kernels: 43.8 us -> 41 us
    pallas_call x1, Pallas kernels: 43.8 us -> 41 us  [on_device(): pl.pallas_call(kernel, out_shape=jax.ShapeDtypeStruct(block, bf16), in_sp...]
where the time goes in v2:
time: 43.3 us; the launch traced here: 43.1 us
  Pallas kernels  41 us (95%)
  other arithmetic  2.15 us (5%)
    pallas_call x1, Pallas kernels, on_device(): pl.pallas_call(kernel, out_shape=jax.ShapeDtypeStruct(block, bf16), in_sp...  41 us
    mul x1, other arithmetic, on_device(): return pressure.astype(f32) * (1.0 / 1024.0)  2.15 us

profile of v2, /device:TPU:1, one launch (start us, length us, event | category | flops | bytes accessed | tf_op | source)
XLA Modules:
  0.0 43.1 jit_solution(10485507275471054101)
XLA Ops:
  0.0 41.0 %poisson.1 = bf16[2,32,32,128]{3,2,1,0:T(8,128)(2,1)} custom-call(bf16[2,32,32,128]{3,2,1,0:T(8,128)(2,1)} %u_hbm.1, bf16[2,32,32,128]{3,2,1,0:T(8,128)(2,1)} %v_hbm.1, bf16[2,32,32,128]{3,2,1,0:T(8,128)(2,1)} %w_hbm.1, f32[64]{0:T(128)} %spacing_hbm.1, s32[8,128]{1,0:T(8,128)} %bitcast.1, s32[32]{0:T(128)} %plane_hbm.1, ...), custom_call_target="tpu_custom_call" | custom-call | tf_op jit(solution)/shard_map/poisson/pallas_call | solution.py:563
  41.0 2.2 %convert_multiply_fusion = f32[2,32,32,128]{3,2,1,0:T(8,128)} fusion(bf16[2,32,32,128]{3,2,1,0:T(8,128)(2,1)} %poisson.1), kind=kLoop, calls=%fused_computation | loop fusion | flops 524288 | bytes 1572864 | tf_op jit(solution)/shard_map/mul | solution.py:632

commit v3 on v2

--- a/solution.py
+++ b/solution.py
@@ -75,8 +75,7 @@
     y_ref[c, rows, 384:512] = (im - im_hi.astype(f32)).astype(bf16)
 
 
-def far_first(i):
-    return lax.rem(2 + i + (i // 2) * (1 + 2 * lax.rem(i, 2)), 4)
+FAR_FIRST = (2, 3, 1, 0)
 
 
 def kernel(
@@ -90,7 +89,22 @@
 ):
     me = lax.axis_index("row")
     g = lax.axis_index("gz")
+    my_y, my_x, my_core = me // 8, lax.rem(me // 2, 4), lax.rem(me, 2)
+    ys = [lax.rem(my_y + d, 4) * 8 for d in FAR_FIRST]
+    ends = [
+        lax.rem(my_x + d, 4) * 2 + lax.rem(my_core + c, 2) for d in FAR_FIRST for c in (1, 0)
+    ]
     barrier = pltpu.get_barrier_semaphore()
+
+    def greet(device):
+        pl.semaphore_signal(barrier, inc=1, device_id=device, device_id_type=MESH)
+
+    for d in (4, 3, 5):
+        greet({"gz": lax.rem(g + d, GZ)})
+    for i in range(ROW - 1):
+        greet({"row": ys[i // 8] + ends[i % 8]})
+    for d in (2, 6, 1, 7):
+        greet({"gz": lax.rem(g + d, GZ)})
     loads = [
         pltpu.make_async_copy(w_hbm, w_v, lsem.at[0]),
         pltpu.make_async_copy(u_hbm, u_v, lsem.at[1]),
@@ -105,21 +119,6 @@
     for load in loads:
         load.start()
 
-    def greet_row(d, carry):
-        pl.semaphore_signal(
-            barrier, inc=1, device_id={"row": lax.rem(me + d, ROW)}, device_id_type=MESH
-        )
-        return carry
-
-    def greet_gz(d, carry):
-        pl.semaphore_signal(
-            barrier, inc=1, device_id={"gz": lax.rem(g + d, GZ)}, device_id_type=MESH
-        )
-        return carry
-
-    lax.fori_loop(1, ROW, greet_row, 0)
-    lax.fori_loop(1, GZ, greet_gz, 0)
-
     def row_send(src, dst, k, t):
         return pltpu.make_async_remote_copy(
             src, dst, bar_send.at[k], bar_recv.at[k], device_id={"row": t}, device_id_type=MESH
@@ -132,14 +131,6 @@
 
     for load in loads[3:]:
         load.wait()
-
-    my_y, my_x, my_core = me // 8, lax.rem(me // 2, 4), lax.rem(me, 2)
-
-    def partner(i):
-        y = lax.rem(my_y + far_first(i // 8), 4)
-        x = lax.rem(my_x + far_first(lax.rem(i // 2, 4)), 4)
-        core = lax.rem(my_core + 1 + lax.rem(i, 2), 2)
-        return (y * 4 + x) * 2 + core
 
     level = level_ref[...]
     width = jnp.zeros((GZ, DEPTH), f32)
@@ -181,12 +172,9 @@
     halo_copy = gz_send(halo_out, halo_in, 0, above)
     halo_copy.start()
 
-    def send_u(i, carry):
-        t = partner(i)
+    for i in range(ROW - 1):
+        t = ys[i // 8] + ends[i % 8]
         row_send(u_v.at[:, t], recv_u.at[:, me], 1, t).start()
-        return carry
-
-    lax.fori_loop(0, ROW - 1, send_u, 0)
     recv_u[:, pl.ds(me, 1)] = u_v[:, pl.ds(me, 1)]
 
     halo_copy.wait()
@@ -222,16 +210,20 @@
             device_id_type=MESH,
         ).start()
 
-    make_source(partner(0))
-
     def source_step(i, carry):
-        make_source(partner(i))
-        send_s(partner(i - 1))
+        base = lax.rem(my_y + lax.rem(2 + i + (i // 2) * (1 + 2 * lax.rem(i, 2)), 4), 4) * 8
+        make_source(base + ends[0])
+        for n in range(1, 8):
+            make_source(base + ends[n])
+            send_s(base + ends[n - 1])
+
+        @pl.when(i < 3)
+        def _():
+            send_s(base + ends[7])
+
         return carry
 
-    lax.fori_loop(1, ROW - 1, source_step, 0)
-    make_source(me)
-    send_s(partner(ROW - 2))
+    lax.fori_loop(0, 4, source_step, 0)
     recv_s[:, pl.ds(me, 1)] = s_v[:, pl.ds(me, 1)]
 
     outer = lax.broadcasted_iota(jnp.int32, (RADIX, 128), 0)
@@ -322,7 +314,7 @@
 
     def forward(recv, ready, finish):
         def flip(i, carry):
-            y = lax.rem(my_y + 4 - far_first(i), 4)
+            y = lax.rem(my_y + 4 - lax.rem(2 + i + (i // 2) * (1 + 2 * lax.rem(i, 2)), 4), 4)
             for n in range(2):
                 ready(2 * y + n)
             for n in range(2):
@@ -333,37 +325,32 @@
 
         lax.fori_loop(0, 4, flip, 0)
 
-        def mix(i, carry):
-            rows = pl.ds(pl.multiple_of(16 * i, 16), 16)
-            xr = [q_t[0, a, rows, :].astype(f32) for a in range(RADIX)]
-            xi = [q_t[1, a, rows, :].astype(f32) for a in range(RADIX)]
-            for c, (re, im) in enumerate(butterfly(xr, xi)):
-                re, im = twisted(re, im, tw_ref, c)
-                put_split(y_s, c, rows, re, im)
-            return carry
-
-        lax.fori_loop(0, DEPTH // 16, mix, 0)
-        for c in range(0, RADIX, 2):
-            finish(c, product(c))
-
-    def product(c):
-        rows = y_s[c : c + 2].reshape(2 * DEPTH, 512)
-        return jnp.dot(rows, weights_ref[0:512, :], preferred_element_type=f32) + jnp.dot(
-            rows[:, 0:256], weights_ref[512:768, :], preferred_element_type=f32
-        )
-
-    def keep_along(c, acc):
-        for n in range(2):
-            kx = kx_s[c + n : c + n + 1, :]
-            own = acc[n * DEPTH : (n + 1) * DEPTH]
-            part[c + n, :, 0:128] = -kx * own[:, 128:256]
-            part[c + n, :, 128:256] = kx * own[:, 0:128]
-
-    def keep_rhs(c, acc):
-        for n in range(2):
-            total = acc[n * DEPTH : (n + 1) * DEPTH] + part[c + n]
-            rhs[0, pl.ds(c + n, DEPTH, stride=8), :] = total[:, 0:128]
-            rhs[1, pl.ds(c + n, DEPTH, stride=8), :] = total[:, 128:256]
+        for half in range(2):
+            for i in range(4):
+                rows = slice(64 * half + 16 * i, 64 * half + 16 * (i + 1))
+                xr = [q_t[0, a, rows, :].astype(f32) for a in range(RADIX)]
+                xi = [q_t[1, a, rows, :].astype(f32) for a in range(RADIX)]
+                for c, (re, im) in enumerate(butterfly(xr, xi)):
+                    re, im = twisted(re, im, tw_ref, c)
+                    put_split(y_s, c, rows, re, im)
+            for c in range(0, RADIX, 4):
+                rows = y_s[c : c + 4, 64 * half : 64 * (half + 1), :].reshape(256, 512)
+                acc = jnp.dot(
+                    rows, weights_ref[0:512, :], preferred_element_type=f32
+                ) + jnp.dot(rows[:, 0:256], weights_ref[512:768, :], preferred_element_type=f32)
+                for n in range(4):
+                    finish(c + n, half, acc[64 * n : 64 * (n + 1)])
+
+    def keep_along(c, half, own):
+        rows = slice(64 * half, 64 * (half + 1))
+        kx = kx_s[c : c + 1, :]
+        part[c, rows, 0:128] = -kx * own[:, 128:256]
+        part[c, rows, 128:256] = kx * own[:, 0:128]
+
+    def keep_rhs(c, half, own):
+        total = own + part[c, 64 * half : 64 * (half + 1)]
+        rhs[0, pl.ds(512 * half + c, 64, stride=8), :] = total[:, 0:128]
+        rhs[1, pl.ds(512 * half + c, 64, stride=8), :] = total[:, 128:256]
 
     def row_wait(ref, k):
         row_send(ref.at[:, 0 : ROW - 1], ref.at[:, 0 : ROW - 1], k, me).wait_recv()
@@ -408,20 +395,38 @@
 
     forward(recv_s, s_ready, keep_rhs)
 
-    def down(i, carry):
-        for h in range(8):
-            j = 8 * i + h
-            out = []
-            for z, pair in ((j, carry[0:2]), (DEPTH - 1 - j, carry[2:4])):
-                inv, fe = inv_s[z], fe_s[z]
-                for n in range(2):
-                    value = rhs[n, at(z), :] * inv - fe * pair[n]
-                    rhs[n, at(z), :] = value
-                    out.append(value)
-            carry = tuple(out)
-        return carry
-
-    low_re, low_im, high_re, high_im = lax.fori_loop(0, HALF // 8, down, (zero,) * 4)
+    def sweep(rows, factor_ref, scale_ref, before):
+        for k in range(0, len(rows), 4):
+            group = rows[k : k + 4]
+            factors = [factor_ref[z] for z in group]
+            products = [-factors[0]]
+            for factor_z in factors[1:]:
+                products.append(-factor_z * products[-1])
+            after = []
+            for n in range(2):
+                partial = None
+                for z, factor_z, product_z in zip(group, factors, products):
+                    own = rhs[n, 8 * z : 8 * z + 8, :]
+                    if scale_ref is not None:
+                        own = own * scale_ref[z]
+                    partial = own if partial is None else own - factor_z * partial
+                    value = partial + product_z * before[n]
+                    rhs[n, 8 * z : 8 * z + 8, :] = value
+                after.append(value)
+            before = after
+            yield before
+
+    def both(low_rows, high_rows, factor_ref, scale_ref, low, high):
+        for low, high in zip(
+            sweep(low_rows, factor_ref, scale_ref, low),
+            sweep(high_rows, factor_ref, scale_ref, high),
+        ):
+            pass
+        return low, high
+
+    (low_re, low_im), (high_re, high_im) = both(
+        range(HALF), range(DEPTH - 1, HALF - 1, -1), fe_s, inv_s, (zero, zero), (zero, zero)
+    )
     bc_low, bc_high = bc_s[HALF - 1], bc_s[HALF]
     inv_det = 1.0 / (1.0 - bc_low * bc_high)
     low_re = (low_re - bc_low * high_re) * inv_det
@@ -433,21 +438,13 @@
     rhs[0, at(HALF), :] = high_re
     rhs[1, at(HALF), :] = high_im
 
-    def up_again(i, carry):
-        for h in range(7):
-            j = 7 * i + h + 1
-            out = []
-            for z, pair in ((HALF - 1 - j, carry[0:2]), (HALF + j, carry[2:4])):
-                bc = bc_s[z]
-                for n in range(2):
-                    value = rhs[n, at(z), :] - bc * pair[n]
-                    rhs[n, at(z), :] = value
-                    out.append(value)
-            carry = tuple(out)
-        return carry
-
-    low_re, low_im, high_re, high_im = lax.fori_loop(
-        0, (HALF - 1) // 7, up_again, (low_re, low_im, high_re, high_im)
+    (low_re, low_im), (high_re, high_im) = both(
+        range(HALF - 2, -1, -1),
+        range(HALF + 1, DEPTH),
+        bc_s,
+        None,
+        (low_re, low_im),
+        (high_re, high_im),
     )
     ex_send[0] = low_re
     ex_send[1] = low_im
@@ -482,23 +479,20 @@
     from_below = [edge[0, n, g] for n in range(2)]
     from_above = [edge[1, n, g] for n in range(2)]
 
-    def correct(i, carry):
-        rows = pl.ds(pl.multiple_of(16 * i, 16), 16)
-        for c in range(RADIX):
-            v_c, w_c = vt_s[c, rows, :], wt_s[c, rows, :]
-            full = [
-                yt_s[n, c, rows, :]
-                + v_c * from_below[n][c : c + 1, :]
-                + w_c * from_above[n][c : c + 1, :]
-                for n in range(2)
-            ]
-            put_split(y_s, c, rows, full[1], full[0])
-        return carry
-
-    lax.fori_loop(0, DEPTH // 16, correct, 0)
+    across = (((1,), (1,)), ((), ()))
     for c in range(0, RADIX, 2):
+        for h in range(2):
+            for i in range(DEPTH // 16):
+                rows = slice(16 * i, 16 * (i + 1))
+                v_c, w_c = vt_s[c + h, rows, :], wt_s[c + h, rows, :]
+                full = [
+                    yt_s[n, c + h, rows, :]
+                    + v_c * from_below[n][c + h : c + h + 1, :]
+                    + w_c * from_above[n][c + h : c + h + 1, :]
+                    for n in range(2)
+                ]
+                put_split(y_s, c + h, rows, full[1], full[0])
         rows = y_s[c : c + 2].reshape(2 * DEPTH, 512)
-        across = (((1,), (1,)), ((), ()))
         acc = lax.dot_general(
             weights_t[:, 0:512], rows, across, preferred_element_type=f32
         ) + lax.dot_general(
@@ -543,10 +537,8 @@
         return carry
 
     lax.fori_loop(1, 4, unmix_step, 0)
-    own = pltpu.make_async_copy(out_v.at[:, me], out_ref.at[:, me], lsem.at[0])
-    own.start()
     give(3, 0)
-    own.wait()
+    out_ref[:, pl.ds(me, 1)] = out_v[:, pl.ds(me, 1)]
     row_wait(out_ref, 5)
     for k, ref in ((1, u_v), (2, s_v), (5, out_v)):
         row_send(ref.at[:, 0 : ROW - 1], ref.at[:, 0 : ROW - 1], k, me).wait_send()
@@ -562,12 +554,12 @@
     tile = (RADIX, DEPTH, 128)
     pressure = pl.pallas_call(
         kernel,
-        out_shape=jax.ShapeDtypeStruct(block, bf16),
+        out_shape=pltpu.VMEM(block, bf16),
         in_specs=[
             pl.BlockSpec(memory_space=pltpu.HBM),
         ]
         * 9,
-        out_specs=pl.BlockSpec(memory_space=pltpu.HBM),
+        out_specs=pl.BlockSpec(memory_space=pltpu.VMEM),
         scratch_shapes=[
             pltpu.SMEM((64,), f32),
             pltpu.VMEM((8, 128), jnp.int32),
@@ -615,19 +607,24 @@
             pltpu.SemaphoreType.DMA((8,)),
         ],
         compiler_params=pltpu.CompilerParams(
-            collective_id=0, has_side_effects=True, vmem_limit_bytes=67043328
+            collective_id=0, has_side_effects=True, vmem_limit_bytes=48 * 1024 * 1024
         ),
         name="poisson",
     )(
-        velocity_x,
-        velocity_y,
-        velocity_z,
-        spacing,
-        level_index.reshape(8, 128),
-        plane_index,
-        jnp.asarray(weights),
-        jnp.asarray(weights.T),
-        jnp.asarray(twiddle),
+        *(
+            pltpu.with_memory_space_constraint(operand, pltpu.HBM)
+            for operand in (
+                velocity_x,
+                velocity_y,
+                velocity_z,
+                spacing,
+                level_index.reshape(8, 128),
+                plane_index,
+                jnp.asarray(weights),
+                jnp.asarray(weights.T),
+                jnp.asarray(twiddle),
+            )
+        )
     )
     return pressure.astype(f32) * (1.0 / 1024.0)
 

time: 43.3 us -> 40.6 us (0.938)
  Pallas kernels: 41 us -> 39.3 us
  other arithmetic: 2.15 us -> 1.11 us
    pallas_call x1, Pallas kernels: 41 us -> 39.3 us  [on_device(): pl.pallas_call(kernel, out_shape=pltpu.VMEM(block, bf16), in_specs=[pl.Bl...]
    mul x1, other arithmetic: 2.15 us -> 1.11 us  [on_device(): return pressure.astype(f32) * (1.0 / 1024.0)]
where the time goes in v3:
time: 40.6 us; the launch traced here: 40.5 us
  Pallas kernels  39.3 us (97%)
  other arithmetic  1.11 us (3%)
    pallas_call x1, Pallas kernels, on_device(): pl.pallas_call(kernel, out_shape=pltpu.VMEM(block, bf16), in_specs=[pl.Bl...  39.3 us
    mul x1, other arithmetic, on_device(): return pressure.astype(f32) * (1.0 / 1024.0)  1.11 us

profile of v3, /device:TPU:1, one launch (start us, length us, event | category | flops | bytes accessed | tf_op | source)
XLA Modules:
  0.0 40.5 jit_solution(1201610964968106224)
XLA Ops:
  0.0 39.3 %poisson.1 = bf16[2,32,32,128]{3,2,1,0:T(8,128)(2,1)S(1)} custom-call(bf16[2,32,32,128]{3,2,1,0:T(8,128)(2,1)} %u_hbm.1, bf16[2,32,32,128]{3,2,1,0:T(8,128)(2,1)} %v_hbm.1, bf16[2,32,32,128]{3,2,1,0:T(8,128)(2,1)} %w_hbm.1, f32[64]{0:T(128)} %spacing_hbm.1, s32[8,128]{1,0:T(8,128)} %bitcast.1, s32[32]{0:T(128)} %plane_hbm.1, ...), custom_call_target="tpu_custom_call" | custom-call | tf_op jit(solution)/shard_map/poisson/pallas_call | solution.py:555
  39.4 1.1 %convert_multiply_fusion = f32[2,32,32,128]{3,2,1,0:T(8,128)} fusion(bf16[2,32,32,128]{3,2,1,0:T(8,128)(2,1)S(1)} %poisson.1), kind=kLoop, calls=%fused_computation | loop fusion | flops 524288 | bytes 1572864 | tf_op jit(solution)/shard_map/mul | solution.py:629

commit v4 on v3

--- a/solution.py
+++ b/solution.py
@@ -76,6 +76,15 @@
 
 
 FAR_FIRST = (2, 3, 1, 0)
+OFFSETS = [(y, x) for y in FAR_FIRST for x in FAR_FIRST]
+
+
+def hops(offset):
+    return sum(min(d, 4 - d) for d in offset)
+
+
+FAR_CHIPS = sorted((d for d in OFFSETS if hops(d) > 2), key=lambda d: -hops(d))
+NEAR_CHIPS = sorted((d for d in OFFSETS if 0 < hops(d) <= 2), key=lambda d: -hops(d))
 
 
 def kernel(
@@ -84,8 +93,8 @@
     spacing_ref, level_ref, plane_ref, weights_ref, weights_t, tw_ref,
     u_v, v_v, w_v, s_v, recv_u, recv_s, out_v, halo_out, halo_in, halo_cols, band, bmat,
     inv_s, fe_s, bc_s, vs_s, ws_s, vt_s, wt_s, yt_s, rhs, part, part_t, tc_s, ts_s, q_t, y_s, kx_s,
-    sp_all, ex_all, sp_send, ex_send, red, edge,
-    lsem, bar_send, bar_recv, s_recv,
+    sp_all, ex_all, sp_send, ex_send, far_send, far_all, red, edge,
+    lsem, bar_send, bar_recv, s_recv, hello,
 ):
     me = lax.axis_index("row")
     g = lax.axis_index("gz")
@@ -95,19 +104,25 @@
         lax.rem(my_x + d, 4) * 2 + lax.rem(my_core + c, 2) for d in FAR_FIRST for c in (1, 0)
     ]
     barrier = pltpu.get_barrier_semaphore()
+    partner = 2 * (me // 2) + 1 - my_core
+    upper_z, lower_z = lax.rem(g + 1, GZ), lax.rem(g + GZ - 1, GZ)
+
+    def chip(d):
+        return lax.rem(my_y + d[0], 4) * 8 + lax.rem(my_x + d[1], 4) * 2
 
     def greet(device):
         pl.semaphore_signal(barrier, inc=1, device_id=device, device_id_type=MESH)
 
-    for d in (4, 3, 5):
-        greet({"gz": lax.rem(g + d, GZ)})
-    for i in range(ROW - 1):
-        greet({"row": ys[i // 8] + ends[i % 8]})
-    for d in (2, 6, 1, 7):
-        greet({"gz": lax.rem(g + d, GZ)})
+    for d in FAR_CHIPS:
+        greet({"row": chip(d) + 1})
+    for d in NEAR_CHIPS:
+        greet({"row": chip(d)})
+    greet({"gz": upper_z})
+    greet({"gz": lower_z})
+    greet({"row": partner})
     loads = [
-        pltpu.make_async_copy(w_hbm, w_v, lsem.at[0]),
-        pltpu.make_async_copy(u_hbm, u_v, lsem.at[1]),
+        pltpu.make_async_copy(u_hbm, u_v, lsem.at[0]),
+        pltpu.make_async_copy(w_hbm, w_v, lsem.at[1]),
         pltpu.make_async_copy(v_hbm, v_v, lsem.at[2]),
         pltpu.make_async_copy(level_hbm, level_ref, lsem.at[3]),
         pltpu.make_async_copy(spacing_hbm, spacing_ref, lsem.at[4]),
@@ -129,8 +144,59 @@
             src, dst, bar_send.at[k], bar_recv.at[k], device_id={"gz": t}, device_id_type=MESH
         )
 
-    for load in loads[3:]:
+    def tell_partner():
+        pl.semaphore_signal(hello.at[4], inc=1, device_id={"row": partner}, device_id_type=MESH)
+
+    def send_u(chips):
+        for n in range(2):
+            for d in chips:
+                t = chip(d) + lax.rem(my_core + 1 + n, 2)
+                row_send(u_v.at[:, t], recv_u.at[:, me], 1, t).start()
+
+    loads[0].wait()
+
+    @pl.when(my_core == 0)
+    def _():
+        pl.semaphore_wait(barrier, 2 * len(NEAR_CHIPS) + 3)
+        tell_partner()
+
+    @pl.when(my_core == 1)
+    def _():
+        pl.semaphore_wait(hello.at[4], 1)
+
+    send_u(NEAR_CHIPS)
+    row_send(u_v.at[:, partner], recv_u.at[:, me], 1, partner).start()
+
+    @pl.when(my_core == 1)
+    def _():
+        pl.semaphore_wait(barrier, 2 * len(FAR_CHIPS) + 3)
+        tell_partner()
+
+    @pl.when(my_core == 0)
+    def _():
+        pl.semaphore_wait(hello.at[4], 1)
+
+    send_u(FAR_CHIPS)
+
+    def greet_z(k, z):
+        pl.semaphore_signal(hello.at[k], inc=1, device_id={"gz": z}, device_id_type=MESH)
+
+    greet_z(0, upper_z)
+    greet_z(1, lower_z)
+    recv_u[:, pl.ds(me, 1)] = u_v[:, pl.ds(me, 1)]
+
+    for load in loads[1:]:
         load.wait()
+
+    pick = (lax.broadcasted_iota(jnp.int32, (16, DEPTH), 1) == DEPTH - 1).astype(f32).astype(bf16)
+    for n in range(2):
+        column = lax.dot_general(
+            pick,
+            w_v[n].reshape(1024, DEPTH),
+            (((1,), (1,)), ((), ())),
+            preferred_element_type=f32,
+        )
+        halo_out[:, n * 1024 : (n + 1) * 1024] = column[0:1, :]
 
     level = level_ref[...]
     width = jnp.zeros((GZ, DEPTH), f32)
@@ -154,39 +220,36 @@
         row_n = jnp.broadcast_to(band[n, pl.ds(g, 1), :], (DEPTH, DEPTH))
         bmat[n] = row_n.T
 
-    loads[0].wait()
-    pick = (lax.broadcasted_iota(jnp.int32, (16, DEPTH), 1) == DEPTH - 1).astype(f32).astype(bf16)
-    for n in range(2):
-        column = lax.dot_general(
-            pick,
-            w_v[n].reshape(1024, DEPTH),
-            (((1,), (1,)), ((), ())),
-            preferred_element_type=f32,
-        )
-        halo_out[:, n * 1024 : (n + 1) * 1024] = column[0:1, :]
-    loads[1].wait()
-    loads[2].wait()
-    pl.semaphore_wait(barrier, ROW - 1 + GZ - 1)
-
-    above = lax.rem(g + 1, GZ)
-    halo_copy = gz_send(halo_out, halo_in, 0, above)
-    halo_copy.start()
-
-    for i in range(ROW - 1):
-        t = ys[i // 8] + ends[i % 8]
-        row_send(u_v.at[:, t], recv_u.at[:, me], 1, t).start()
-    recv_u[:, pl.ds(me, 1)] = u_v[:, pl.ds(me, 1)]
-
-    halo_copy.wait()
-    has_below = jnp.where(g > 0, 1.0, 0.0)
+    halo_copy = gz_send(halo_out, halo_in, 0, upper_z)
+
+    @pl.when(g < GZ - 1)
+    def _():
+        halo_copy.start()
+
+    @pl.when(g == 0)
+    def _():
+        halo_in[...] = jnp.zeros_like(halo_in)
+
+    @pl.when(g > 0)
+    def _():
+        halo_copy.wait_recv()
+
+    @pl.when(g < GZ - 1)
+    def _():
+        halo_copy.wait_send()
+
     first_lane = (lax.broadcasted_iota(jnp.int32, (8, DEPTH), 1) == 0).astype(f32)
     first_row = (lax.broadcasted_iota(jnp.int32, (8, DEPTH), 0) == 0).astype(f32)
-    spot = (first_lane * first_row * has_below).astype(bf16)
+    spot = (first_lane * first_row).astype(bf16)
     for n in range(2):
         wide = jnp.broadcast_to(halo_in[:, n * 1024 : (n + 1) * 1024], (8, 1024)).astype(bf16)
         halo_cols[n] = lax.dot_general(
             wide, spot, (((0,), (0,)), ((), ())), preferred_element_type=f32
         ).reshape(32, 32, DEPTH)
+    pl.semaphore_wait(hello.at[0], 1)
+    pl.semaphore_wait(hello.at[1], 1)
+    greet_z(2, lax.rem(g + 2, GZ))
+    greet_z(3, lax.rem(g + GZ - 2, GZ))
     inv_width = band[3, pl.ds(g, 1), :]
     lane32 = lax.broadcasted_iota(jnp.int32, (32, DEPTH), 1)
 
@@ -305,6 +368,9 @@
         vt_s[c] = vs_s[pl.ds(c, DEPTH, stride=8), :]
         wt_s[c] = ws_s[pl.ds(c, DEPTH, stride=8), :]
 
+    pl.semaphore_wait(hello.at[2], 1)
+    pl.semaphore_wait(hello.at[3], 1)
+
     def send_sp(d, carry):
         t = lax.rem(g + d, GZ)
         gz_send(sp_send, sp_all.at[g], 3, t).start()
@@ -446,18 +512,31 @@
         (low_re, low_im),
         (high_re, high_im),
     )
+    far_send[0, 0:8] = low_re.astype(bf16)
+    far_send[0, 8:16] = low_im.astype(bf16)
+    far_send[1, 0:8] = high_re.astype(bf16)
+    far_send[1, 8:16] = high_im.astype(bf16)
     ex_send[0] = low_re
     ex_send[1] = low_im
     ex_send[2] = high_re
     ex_send[3] = high_im
     ex_all[pl.ds(g, 1)] = ex_send[...][None]
 
-    for d in (4, 3, 5, 2, 6, 1, 7):
+    for d in (4, 3, 5):
+        gz_send(far_send, far_all.at[g], 6, lax.rem(g + d, GZ)).start()
+    for d in (2, 6, 1, 7):
         gz_send(ex_send, ex_all.at[g], 4, lax.rem(g + d, GZ)).start()
     for c in range(RADIX):
         for n in range(2):
             yt_s[n, c] = rhs[n, pl.ds(c, DEPTH, stride=8), :]
-    gz_send(ex_all.at[0 : GZ - 1], ex_all.at[0 : GZ - 1], 4, g).wait_recv()
+    gz_send(ex_all.at[0:4], ex_all.at[0:4], 4, g).wait_recv()
+    gz_send(far_all.at[0:3], far_all.at[0:3], 6, g).wait_recv()
+    for d in (3, 4, 5):
+        b = lax.rem(g + d, GZ)
+        for n in range(2):
+            pair = far_all[b, n].astype(f32)
+            ex_all[b, 2 * n] = pair[0:8]
+            ex_all[b, 2 * n + 1] = pair[8:16]
 
     for n in range(2):
         alpha = zero
@@ -502,21 +581,19 @@
             for h in range(2):
                 part_t[n, c + h] = acc[n * 128 : (n + 1) * 128, h * DEPTH : (h + 1) * DEPTH]
 
-    def unmix(q, carry):
-        for h in range(2):
-            rows = pl.ds(pl.multiple_of(32 * q + 16 * h, 16), 16)
-            turned = []
-            for c in range(RADIX):
-                re, im = part_t[0, c, rows, :], part_t[1, c, rows, :]
-                if c > 0:
-                    cos, sin = tc_s[c, rows, :], ts_s[c, rows, :]
-                    re, im = re * cos + im * sin, im * cos - re * sin
-                turned.append((re, im))
-            mixed = butterfly([t[0] for t in turned], [t[1] for t in turned])
-            for j, (first, second) in enumerate(mixed):
-                out_v[0, 4 * j + q, 16 * h : 16 * h + 16, :] = second.astype(bf16)
-                out_v[1, 4 * j + q, 16 * h : 16 * h + 16, :] = first.astype(bf16)
-        return carry
+    def unmix(q, h):
+        rows = pl.ds(pl.multiple_of(32 * q + 16 * h, 16), 16)
+        turned = []
+        for c in range(RADIX):
+            re, im = part_t[0, c, rows, :], part_t[1, c, rows, :]
+            if c > 0:
+                cos, sin = tc_s[c, rows, :], ts_s[c, rows, :]
+                re, im = re * cos + im * sin, im * cos - re * sin
+            turned.append((re, im))
+        mixed = butterfly([t[0] for t in turned], [t[1] for t in turned])
+        for j, (first, second) in enumerate(mixed):
+            out_v[0, 4 * j + q, 16 * h : 16 * h + 16, :] = second.astype(bf16)
+            out_v[1, 4 * j + q, 16 * h : 16 * h + 16, :] = first.astype(bf16)
 
     def give(q, carry):
         for i in range(RADIX):
@@ -530,10 +607,12 @@
         return carry
 
     unmix(0, 0)
+    unmix(0, 1)
 
     def unmix_step(q, carry):
-        unmix(q, carry)
+        unmix(q, 0)
         give(q - 1, carry)
+        unmix(q, 1)
         return carry
 
     lax.fori_loop(1, 4, unmix_step, 0)
@@ -542,8 +621,8 @@
     row_wait(out_ref, 5)
     for k, ref in ((1, u_v), (2, s_v), (5, out_v)):
         row_send(ref.at[:, 0 : ROW - 1], ref.at[:, 0 : ROW - 1], k, me).wait_send()
-    for k, ref in ((3, sp_all), (4, ex_all)):
-        gz_send(ref.at[0 : GZ - 1], ref.at[0 : GZ - 1], k, g).wait_send()
+    for k, ref, n in ((3, sp_all, 7), (4, ex_all, 4), (6, far_all, 3)):
+        gz_send(ref.at[0:n], ref.at[0:n], k, g).wait_send()
 
 
 def on_device(velocity_x, velocity_y, velocity_z, spacing, level_index, plane_index):
@@ -599,12 +678,15 @@
             pltpu.VMEM((GZ, 4, RADIX, 128), f32),
             pltpu.VMEM((4, RADIX, 128), f32),
             pltpu.VMEM((4, RADIX, 128), f32),
+            pltpu.VMEM((2, 2 * RADIX, 128), bf16),
+            pltpu.VMEM((GZ, 2, 2 * RADIX, 128), bf16),
             pltpu.VMEM((6, GZ, RADIX, 128), f32),
             pltpu.VMEM((2, 2, GZ, RADIX, 128), f32),
             pltpu.SemaphoreType.DMA((9,)),
-            pltpu.SemaphoreType.DMA((6,)),
-            pltpu.SemaphoreType.DMA((6,)),
+            pltpu.SemaphoreType.DMA((7,)),
+            pltpu.SemaphoreType.DMA((7,)),
             pltpu.SemaphoreType.DMA((8,)),
+            pltpu.SemaphoreType.REGULAR((5,)),
         ],
         compiler_params=pltpu.CompilerParams(
             collective_id=0, has_side_effects=True, vmem_limit_bytes=48 * 1024 * 1024

time: 40.6 us -> 40.4 us (level)
  no operation moved by 1% of the time
where the time goes in v4:
time: 40.4 us; the launch traced here: 40.3 us
  Pallas kernels  39.2 us (97%)
  other arithmetic  1.11 us (3%)
    pallas_call x1, Pallas kernels, on_device(): pl.pallas_call(kernel, out_shape=pltpu.VMEM(block, bf16), in_specs=[pl.Bl...  39.2 us
    mul x1, other arithmetic, on_device(): return pressure.astype(f32) * (1.0 / 1024.0)  1.11 us

profile of v4, /device:TPU:1, one launch (start us, length us, event | category | flops | bytes accessed | tf_op | source)
XLA Modules:
  0.0 40.3 jit_solution(13590982796465015086)
XLA Ops:
  0.0 39.2 %poisson.1 = bf16[2,32,32,128]{3,2,1,0:T(8,128)(2,1)S(1)} custom-call(bf16[2,32,32,128]{3,2,1,0:T(8,128)(2,1)} %u_hbm.1, bf16[2,32,32,128]{3,2,1,0:T(8,128)(2,1)} %v_hbm.1, bf16[2,32,32,128]{3,2,1,0:T(8,128)(2,1)} %w_hbm.1, f32[64]{0:T(128)} %spacing_hbm.1, s32[8,128]{1,0:T(8,128)} %bitcast.1, s32[32]{0:T(128)} %plane_hbm.1, ...), custom_call_target="tpu_custom_call" | custom-call | tf_op jit(solution)/shard_map/poisson/pallas_call | solution.py:634
  39.2 1.1 %convert_multiply_fusion = f32[2,32,32,128]{3,2,1,0:T(8,128)} fusion(bf16[2,32,32,128]{3,2,1,0:T(8,128)(2,1)S(1)} %poisson.1), kind=kLoop, calls=%fused_computation | loop fusion | flops 524288 | bytes 1572864 | tf_op jit(solution)/shard_map/mul | solution.py:711

commit v5 on v4

--- a/solution.py
+++ b/solution.py
@@ -99,10 +99,6 @@
     me = lax.axis_index("row")
     g = lax.axis_index("gz")
     my_y, my_x, my_core = me // 8, lax.rem(me // 2, 4), lax.rem(me, 2)
-    ys = [lax.rem(my_y + d, 4) * 8 for d in FAR_FIRST]
-    ends = [
-        lax.rem(my_x + d, 4) * 2 + lax.rem(my_core + c, 2) for d in FAR_FIRST for c in (1, 0)
-    ]
     barrier = pltpu.get_barrier_semaphore()
     partner = 2 * (me // 2) + 1 - my_core
     upper_z, lower_z = lax.rem(g + 1, GZ), lax.rem(g + GZ - 1, GZ)
@@ -147,11 +143,10 @@
     def tell_partner():
         pl.semaphore_signal(hello.at[4], inc=1, device_id={"row": partner}, device_id_type=MESH)
 
-    def send_u(chips):
-        for n in range(2):
-            for d in chips:
-                t = chip(d) + lax.rem(my_core + 1 + n, 2)
-                row_send(u_v.at[:, t], recv_u.at[:, me], 1, t).start()
+    def send_u(chips, core):
+        for d in chips:
+            t = chip(d) + core
+            row_send(u_v.at[:, t], recv_u.at[:, me], 1, t).start()
 
     loads[0].wait()
 
@@ -164,7 +159,8 @@
     def _():
         pl.semaphore_wait(hello.at[4], 1)
 
-    send_u(NEAR_CHIPS)
+    send_u(NEAR_CHIPS, 0)
+    send_u(NEAR_CHIPS, 1)
     row_send(u_v.at[:, partner], recv_u.at[:, me], 1, partner).start()
 
     @pl.when(my_core == 1)
@@ -176,7 +172,7 @@
     def _():
         pl.semaphore_wait(hello.at[4], 1)
 
-    send_u(FAR_CHIPS)
+    send_u(FAR_CHIPS, 0)
 
     def greet_z(k, z):
         pl.semaphore_signal(hello.at[k], inc=1, device_id={"gz": z}, device_id_type=MESH)
@@ -229,65 +225,6 @@
     @pl.when(g == 0)
     def _():
         halo_in[...] = jnp.zeros_like(halo_in)
-
-    @pl.when(g > 0)
-    def _():
-        halo_copy.wait_recv()
-
-    @pl.when(g < GZ - 1)
-    def _():
-        halo_copy.wait_send()
-
-    first_lane = (lax.broadcasted_iota(jnp.int32, (8, DEPTH), 1) == 0).astype(f32)
-    first_row = (lax.broadcasted_iota(jnp.int32, (8, DEPTH), 0) == 0).astype(f32)
-    spot = (first_lane * first_row).astype(bf16)
-    for n in range(2):
-        wide = jnp.broadcast_to(halo_in[:, n * 1024 : (n + 1) * 1024], (8, 1024)).astype(bf16)
-        halo_cols[n] = lax.dot_general(
-            wide, spot, (((0,), (0,)), ((), ())), preferred_element_type=f32
-        ).reshape(32, 32, DEPTH)
-    pl.semaphore_wait(hello.at[0], 1)
-    pl.semaphore_wait(hello.at[1], 1)
-    greet_z(2, lax.rem(g + 2, GZ))
-    greet_z(3, lax.rem(g + GZ - 2, GZ))
-    inv_width = band[3, pl.ds(g, 1), :]
-    lane32 = lax.broadcasted_iota(jnp.int32, (32, DEPTH), 1)
-
-    def make_source(t):
-        wave = plane_ref[t].astype(f32) * wave_unit
-        slopes = []
-        for n in range(2):
-            upward = w_v[n, t].astype(f32)
-            below = jnp.where(lane32 == 0, halo_cols[n, t], pltpu.roll(upward, 1, 1))
-            slopes.append((upward - below) * inv_width)
-        s_v[0, t] = (-wave * v_v[1, t].astype(f32) + slopes[0]).astype(bf16)
-        s_v[1, t] = (wave * v_v[0, t].astype(f32) + slopes[1]).astype(bf16)
-
-    def send_s(t):
-        pltpu.make_async_remote_copy(
-            s_v.at[:, t],
-            recv_s.at[:, me],
-            bar_send.at[2],
-            s_recv.at[me // 4],
-            device_id={"row": t},
-            device_id_type=MESH,
-        ).start()
-
-    def source_step(i, carry):
-        base = lax.rem(my_y + lax.rem(2 + i + (i // 2) * (1 + 2 * lax.rem(i, 2)), 4), 4) * 8
-        make_source(base + ends[0])
-        for n in range(1, 8):
-            make_source(base + ends[n])
-            send_s(base + ends[n - 1])
-
-        @pl.when(i < 3)
-        def _():
-            send_s(base + ends[7])
-
-        return carry
-
-    lax.fori_loop(0, 4, source_step, 0)
-    recv_s[:, pl.ds(me, 1)] = s_v[:, pl.ds(me, 1)]
 
     outer = lax.broadcasted_iota(jnp.int32, (RADIX, 128), 0)
     inner = lax.broadcasted_iota(jnp.int32, (RADIX, 128), 1)
@@ -368,6 +305,72 @@
         vt_s[c] = vs_s[pl.ds(c, DEPTH, stride=8), :]
         wt_s[c] = ws_s[pl.ds(c, DEPTH, stride=8), :]
 
+    @pl.when(g > 0)
+    def _():
+        halo_copy.wait_recv()
+
+    @pl.when(g < GZ - 1)
+    def _():
+        halo_copy.wait_send()
+
+    first_lane = (lax.broadcasted_iota(jnp.int32, (8, DEPTH), 1) == 0).astype(f32)
+    first_row = (lax.broadcasted_iota(jnp.int32, (8, DEPTH), 0) == 0).astype(f32)
+    spot = (first_lane * first_row).astype(bf16)
+    for n in range(2):
+        wide = jnp.broadcast_to(halo_in[:, n * 1024 : (n + 1) * 1024], (8, 1024)).astype(bf16)
+        halo_cols[n] = lax.dot_general(
+            wide, spot, (((0,), (0,)), ((), ())), preferred_element_type=f32
+        ).reshape(32, 32, DEPTH)
+    pl.semaphore_wait(hello.at[0], 1)
+    pl.semaphore_wait(hello.at[1], 1)
+    greet_z(2, lax.rem(g + 2, GZ))
+    greet_z(3, lax.rem(g + GZ - 2, GZ))
+    inv_width = band[3, pl.ds(g, 1), :]
+    lane32 = lax.broadcasted_iota(jnp.int32, (32, DEPTH), 1)
+
+    def make_source(t):
+        wave = plane_ref[t].astype(f32) * wave_unit
+        slopes = []
+        for n in range(2):
+            upward = w_v[n, t].astype(f32)
+            below = jnp.where(lane32 == 0, halo_cols[n, t], pltpu.roll(upward, 1, 1))
+            slopes.append((upward - below) * inv_width)
+        s_v[0, t] = (-wave * v_v[1, t].astype(f32) + slopes[0]).astype(bf16)
+        s_v[1, t] = (wave * v_v[0, t].astype(f32) + slopes[1]).astype(bf16)
+
+    def send_s(t):
+        pltpu.make_async_remote_copy(
+            s_v.at[:, t],
+            recv_s.at[:, me],
+            bar_send.at[2],
+            s_recv.at[me // 4],
+            device_id={"row": t},
+            device_id_type=MESH,
+        ).start()
+
+    columns = [lax.rem(my_x + d, 4) * 2 for d in FAR_FIRST]
+
+    def sources_for(core):
+        def source_step(i, carry):
+            base = lax.rem(my_y + lax.rem(2 + i + (i // 2) * (1 + 2 * lax.rem(i, 2)), 4), 4) * 8
+            make_source(base + columns[0] + core)
+            for n in range(1, 4):
+                make_source(base + columns[n] + core)
+                send_s(base + columns[n - 1] + core)
+
+            @pl.when(base + columns[3] + core != me)
+            def _():
+                send_s(base + columns[3] + core)
+
+            return carry
+
+        lax.fori_loop(0, 4, source_step, 0)
+
+    sources_for(0)
+    send_u(FAR_CHIPS, 1)
+    sources_for(1)
+    recv_s[:, pl.ds(me, 1)] = s_v[:, pl.ds(me, 1)]
+
     pl.semaphore_wait(hello.at[2], 1)
     pl.semaphore_wait(hello.at[3], 1)
 
@@ -429,20 +432,6 @@
     lax.fori_loop(1, RADIX, turn_table, 0)
     row_wait(recv_u, 1)
     forward(recv_u, lambda a: None, keep_along)
-
-    gz_send(sp_all.at[0 : GZ - 1], sp_all.at[0 : GZ - 1], 3, g).wait_recv()
-    beta = zero
-    for b in range(GZ):
-        v_first, v_last, w_first, w_last = (sp_all[b, n] for n in range(4))
-        inv = 1.0 / (1.0 - v_first * beta)
-        gamma = v_last * beta * inv
-        red[0, b] = gamma
-        red[1, b] = v_last + gamma * v_first
-        red[2, b] = inv
-        red[3, b] = inv * v_first
-        red[4, b] = inv * w_first
-        beta = w_last + gamma * w_first
-        red[5, b] = beta
 
     def s_ready(a):
         def wait_for(count):
@@ -529,6 +518,20 @@
     for c in range(RADIX):
         for n in range(2):
             yt_s[n, c] = rhs[n, pl.ds(c, DEPTH, stride=8), :]
+    gz_send(sp_all.at[0 : GZ - 1], sp_all.at[0 : GZ - 1], 3, g).wait_recv()
+    beta = zero
+    for b in range(GZ):
+        v_first, v_last, w_first, w_last = (sp_all[b, n] for n in range(4))
+        inv = 1.0 / (1.0 - v_first * beta)
+        gamma = v_last * beta * inv
+        red[0, b] = gamma
+        red[1, b] = v_last + gamma * v_first
+        red[2, b] = inv
+        red[3, b] = inv * v_first
+        red[4, b] = inv * w_first
+        beta = w_last + gamma * w_first
+        red[5, b] = beta
+
     gz_send(ex_all.at[0:4], ex_all.at[0:4], 4, g).wait_recv()
     gz_send(far_all.at[0:3], far_all.at[0:3], 6, g).wait_recv()
     for d in (3, 4, 5):
@@ -606,13 +609,16 @@
 
         return carry
 
+    def turn(i):
+        return 2 * lax.rem(i, 2) + i // 2
+
     unmix(0, 0)
     unmix(0, 1)
 
-    def unmix_step(q, carry):
-        unmix(q, 0)
-        give(q - 1, carry)
-        unmix(q, 1)
+    def unmix_step(i, carry):
+        unmix(turn(i), 0)
+        give(turn(i - 1), carry)
+        unmix(turn(i), 1)
         return carry
 
     lax.fori_loop(1, 4, unmix_step, 0)

time: 40.4 us -> 39.6 us (0.980)
  Pallas kernels: 39.2 us -> 38.4 us
    pallas_call x1, Pallas kernels: 39.2 us -> 38.4 us  [on_device(): pl.pallas_call(kernel, out_shape=pltpu.VMEM(block, bf16), in_specs=[pl.Bl...]
where the time goes in v5:
time: 39.6 us; the launch traced here: 39.5 us
  Pallas kernels  38.4 us (97%)
  other arithmetic  1.11 us (3%)
    pallas_call x1, Pallas kernels, on_device(): pl.pallas_call(kernel, out_shape=pltpu.VMEM(block, bf16), in_specs=[pl.Bl...  38.4 us
    mul x1, other arithmetic, on_device(): return pressure.astype(f32) * (1.0 / 1024.0)  1.11 us

profile of v5, /device:TPU:1, one launch (start us, length us, event | category | flops | bytes accessed | tf_op | source)
XLA Modules:
  0.0 39.5 jit_solution(1312441168947945810)
XLA Ops:
  0.0 38.4 %poisson.1 = bf16[2,32,32,128]{3,2,1,0:T(8,128)(2,1)S(1)} custom-call(bf16[2,32,32,128]{3,2,1,0:T(8,128)(2,1)} %u_hbm.1, bf16[2,32,32,128]{3,2,1,0:T(8,128)(2,1)} %v_hbm.1, bf16[2,32,32,128]{3,2,1,0:T(8,128)(2,1)} %w_hbm.1, f32[64]{0:T(128)} %spacing_hbm.1, s32[8,128]{1,0:T(8,128)} %bitcast.1, s32[32]{0:T(128)} %plane_hbm.1, ...), custom_call_target="tpu_custom_call" | custom-call | tf_op jit(solution)/shard_map/poisson/pallas_call | solution.py:640
  38.4 1.1 %convert_multiply_fusion = f32[2,32,32,128]{3,2,1,0:T(8,128)} fusion(bf16[2,32,32,128]{3,2,1,0:T(8,128)(2,1)S(1)} %poisson.1), kind=kLoop, calls=%fused_computation | loop fusion | flops 524288 | bytes 1572864 | tf_op jit(solution)/shard_map/mul | solution.py:717

commit v6 on v5

--- a/solution.py
+++ b/solution.py
@@ -113,8 +113,8 @@
         greet({"row": chip(d) + 1})
     for d in NEAR_CHIPS:
         greet({"row": chip(d)})
-    greet({"gz": upper_z})
-    greet({"gz": lower_z})
+    greet({"row": 2 * (me // 2), "gz": upper_z})
+    greet({"row": 2 * (me // 2), "gz": lower_z})
     greet({"row": partner})
     loads = [
         pltpu.make_async_copy(u_hbm, u_v, lsem.at[0]),
@@ -152,7 +152,7 @@
 
     @pl.when(my_core == 0)
     def _():
-        pl.semaphore_wait(barrier, 2 * len(NEAR_CHIPS) + 3)
+        pl.semaphore_wait(barrier, 2 * len(NEAR_CHIPS) + 5)
         tell_partner()
 
     @pl.when(my_core == 1)
@@ -163,26 +163,7 @@
     send_u(NEAR_CHIPS, 1)
     row_send(u_v.at[:, partner], recv_u.at[:, me], 1, partner).start()
 
-    @pl.when(my_core == 1)
-    def _():
-        pl.semaphore_wait(barrier, 2 * len(FAR_CHIPS) + 3)
-        tell_partner()
-
-    @pl.when(my_core == 0)
-    def _():
-        pl.semaphore_wait(hello.at[4], 1)
-
-    send_u(FAR_CHIPS, 0)
-
-    def greet_z(k, z):
-        pl.semaphore_signal(hello.at[k], inc=1, device_id={"gz": z}, device_id_type=MESH)
-
-    greet_z(0, upper_z)
-    greet_z(1, lower_z)
-    recv_u[:, pl.ds(me, 1)] = u_v[:, pl.ds(me, 1)]
-
-    for load in loads[1:]:
-        load.wait()
+    loads[1].wait()
 
     pick = (lax.broadcasted_iota(jnp.int32, (16, DEPTH), 1) == DEPTH - 1).astype(f32).astype(bf16)
     for n in range(2):
@@ -193,6 +174,37 @@
             preferred_element_type=f32,
         )
         halo_out[:, n * 1024 : (n + 1) * 1024] = column[0:1, :]
+
+    halo_copy = gz_send(halo_out, halo_in, 0, upper_z)
+
+    @pl.when(g < GZ - 1)
+    def _():
+        halo_copy.start()
+
+    @pl.when(g == 0)
+    def _():
+        halo_in[...] = jnp.zeros_like(halo_in)
+
+    @pl.when(my_core == 1)
+    def _():
+        pl.semaphore_wait(barrier, 2 * len(FAR_CHIPS) + 1)
+        tell_partner()
+
+    @pl.when(my_core == 0)
+    def _():
+        pl.semaphore_wait(hello.at[4], 1)
+
+    send_u(FAR_CHIPS, 0)
+
+    def greet_z(k, z):
+        pl.semaphore_signal(hello.at[k], inc=1, device_id={"gz": z}, device_id_type=MESH)
+
+    greet_z(0, upper_z)
+    greet_z(1, lower_z)
+    recv_u[:, pl.ds(me, 1)] = u_v[:, pl.ds(me, 1)]
+
+    for load in loads[2:]:
+        load.wait()
 
     level = level_ref[...]
     width = jnp.zeros((GZ, DEPTH), f32)
@@ -215,16 +227,6 @@
     for n in range(3):
         row_n = jnp.broadcast_to(band[n, pl.ds(g, 1), :], (DEPTH, DEPTH))
         bmat[n] = row_n.T
-
-    halo_copy = gz_send(halo_out, halo_in, 0, upper_z)
-
-    @pl.when(g < GZ - 1)
-    def _():
-        halo_copy.start()
-
-    @pl.when(g == 0)
-    def _():
-        halo_in[...] = jnp.zeros_like(halo_in)
 
     outer = lax.broadcasted_iota(jnp.int32, (RADIX, 128), 0)
     inner = lax.broadcasted_iota(jnp.int32, (RADIX, 128), 1)

time: 39.6 us -> 39.1 us (0.987)
  Pallas kernels: 38.4 us -> 37.9 us
    pallas_call x1, Pallas kernels: 38.4 us -> 37.9 us  [on_device(): pl.pallas_call(kernel, out_shape=pltpu.VMEM(block, bf16), in_specs=[pl.Bl...]
where the time goes in v6:
time: 39.1 us; the launch traced here: 39 us
  Pallas kernels  37.9 us (97%)
  other arithmetic  1.11 us (3%)
    pallas_call x1, Pallas kernels, on_device(): pl.pallas_call(kernel, out_shape=pltpu.VMEM(block, bf16), in_specs=[pl.Bl...  37.9 us
    mul x1, other arithmetic, on_device(): return pressure.astype(f32) * (1.0 / 1024.0)  1.11 us

profile of v6, /device:TPU:1, one launch (start us, length us, event | category | flops | bytes accessed | tf_op | source)
XLA Modules:
  0.0 39.0 jit_solution(2862382480141077995)
XLA Ops:
  0.0 37.9 %poisson.1 = bf16[2,32,32,128]{3,2,1,0:T(8,128)(2,1)S(1)} custom-call(bf16[2,32,32,128]{3,2,1,0:T(8,128)(2,1)} %u_hbm.1, bf16[2,32,32,128]{3,2,1,0:T(8,128)(2,1)} %v_hbm.1, bf16[2,32,32,128]{3,2,1,0:T(8,128)(2,1)} %w_hbm.1, f32[64]{0:T(128)} %spacing_hbm.1, s32[8,128]{1,0:T(8,128)} %bitcast.1, s32[32]{0:T(128)} %plane_hbm.1, ...), custom_call_target="tpu_custom_call" | custom-call | tf_op jit(solution)/shard_map/poisson/pallas_call | solution.py:642
  37.9 1.1 %convert_multiply_fusion = f32[2,32,32,128]{3,2,1,0:T(8,128)} fusion(bf16[2,32,32,128]{3,2,1,0:T(8,128)(2,1)S(1)} %poisson.1), kind=kLoop, calls=%fused_computation | loop fusion | flops 524288 | bytes 1572864 | tf_op jit(solution)/shard_map/mul | solution.py:719

commit v7 on v6

--- a/solution.py
+++ b/solution.py
@@ -612,10 +612,10 @@
         return carry
 
     def turn(i):
-        return 2 * lax.rem(i, 2) + i // 2
-
-    unmix(0, 0)
-    unmix(0, 1)
+        return lax.rem(i, 2) * 2 + 1 - i // 2
+
+    unmix(turn(0), 0)
+    unmix(turn(0), 1)
 
     def unmix_step(i, carry):
         unmix(turn(i), 0)
@@ -624,7 +624,7 @@
         return carry
 
     lax.fori_loop(1, 4, unmix_step, 0)
-    give(3, 0)
+    give(turn(3), 0)
     out_ref[:, pl.ds(me, 1)] = out_v[:, pl.ds(me, 1)]
     row_wait(out_ref, 5)
     for k, ref in ((1, u_v), (2, s_v), (5, out_v)):

time: 39.1 us -> 38.2 us (0.977)
  Pallas kernels: 37.9 us -> 36.8 us
    pallas_call x1, Pallas kernels: 37.9 us -> 36.8 us  [on_device(): pl.pallas_call(kernel, out_shape=pltpu.VMEM(block, bf16), in_specs=[pl.Bl...]
where the time goes in v7:
time: 38.2 us; the launch traced here: 37.9 us
  Pallas kernels  36.8 us (96%)
  other arithmetic  1.11 us (3%)
    pallas_call x1, Pallas kernels, on_device(): pl.pallas_call(kernel, out_shape=pltpu.VMEM(block, bf16), in_specs=[pl.Bl...  36.8 us
    mul x1, other arithmetic, on_device(): return pressure.astype(f32) * (1.0 / 1024.0)  1.11 us

profile of v7, /device:TPU:1, one launch (start us, length us, event | category | flops | bytes accessed | tf_op | source)
XLA Modules:
  0.0 37.9 jit_solution(5319437859610917843)
XLA Ops:
  0.0 36.8 %poisson.1 = bf16[2,32,32,128]{3,2,1,0:T(8,128)(2,1)S(1)} custom-call(bf16[2,32,32,128]{3,2,1,0:T(8,128)(2,1)} %u_hbm.1, bf16[2,32,32,128]{3,2,1,0:T(8,128)(2,1)} %v_hbm.1, bf16[2,32,32,128]{3,2,1,0:T(8,128)(2,1)} %w_hbm.1, f32[64]{0:T(128)} %spacing_hbm.1, s32[8,128]{1,0:T(8,128)} %bitcast.1, s32[32]{0:T(128)} %plane_hbm.1, ...), custom_call_target="tpu_custom_call" | custom-call | tf_op jit(solution)/shard_map/poisson/pallas_call | solution.py:642
  36.8 1.1 %convert_multiply_fusion = f32[2,32,32,128]{3,2,1,0:T(8,128)} fusion(bf16[2,32,32,128]{3,2,1,0:T(8,128)(2,1)S(1)} %poisson.1), kind=kLoop, calls=%fused_computation | loop fusion | flops 524288 | bytes 1572864 | tf_op jit(solution)/shard_map/mul | solution.py:719

commit v8 on v7

--- a/solution.py
+++ b/solution.py
@@ -340,11 +340,11 @@
         s_v[0, t] = (-wave * v_v[1, t].astype(f32) + slopes[0]).astype(bf16)
         s_v[1, t] = (wave * v_v[0, t].astype(f32) + slopes[1]).astype(bf16)
 
-    def send_s(t):
+    def send_s(t, core):
         pltpu.make_async_remote_copy(
             s_v.at[:, t],
             recv_s.at[:, me],
-            bar_send.at[2],
+            bar_send.at[2 + 5 * core],
             s_recv.at[me // 4],
             device_id={"row": t},
             device_id_type=MESH,
@@ -352,25 +352,40 @@
 
     columns = [lax.rem(my_x + d, 4) * 2 for d in FAR_FIRST]
 
-    def sources_for(core):
+    def sources_for(core, with_sends):
         def source_step(i, carry):
             base = lax.rem(my_y + lax.rem(2 + i + (i // 2) * (1 + 2 * lax.rem(i, 2)), 4), 4) * 8
-            make_source(base + columns[0] + core)
-            for n in range(1, 4):
-                make_source(base + columns[n] + core)
-                send_s(base + columns[n - 1] + core)
+            for n in range(4):
+                if with_sends:
+                    make_source(base + columns[n] + core)
+                if n > 0:
+                    send_s(base + columns[n - 1] + core, core)
 
             @pl.when(base + columns[3] + core != me)
             def _():
-                send_s(base + columns[3] + core)
+                send_s(base + columns[3] + core, core)
 
             return carry
 
         lax.fori_loop(0, 4, source_step, 0)
 
-    sources_for(0)
+    def s_sent(k, count):
+        row_send(s_v.at[:, 0:count], recv_s.at[:, 0:count], k, me).wait_send()
+
+    sources_for(0, True)
+    def source_ahead(i, carry):
+        make_source(2 * i + 1)
+        return carry
+
+    lax.fori_loop(0, 16, source_ahead, 0)
+    for core in range(2):
+
+        @pl.when(my_core == core)
+        def _():
+            s_sent(2, 15 + core)
+
     send_u(FAR_CHIPS, 1)
-    sources_for(1)
+    sources_for(1, False)
     recv_s[:, pl.ds(me, 1)] = s_v[:, pl.ds(me, 1)]
 
     pl.semaphore_wait(hello.at[2], 1)
@@ -627,7 +642,13 @@
     give(turn(3), 0)
     out_ref[:, pl.ds(me, 1)] = out_v[:, pl.ds(me, 1)]
     row_wait(out_ref, 5)
-    for k, ref in ((1, u_v), (2, s_v), (5, out_v)):
+    for core in range(2):
+
+        @pl.when(my_core == core)
+        def _():
+            s_sent(7, 16 - core)
+
+    for k, ref in ((1, u_v), (5, out_v)):
         row_send(ref.at[:, 0 : ROW - 1], ref.at[:, 0 : ROW - 1], k, me).wait_send()
     for k, ref, n in ((3, sp_all, 7), (4, ex_all, 4), (6, far_all, 3)):
         gz_send(ref.at[0:n], ref.at[0:n], k, g).wait_send()
@@ -691,8 +712,8 @@
             pltpu.VMEM((6, GZ, RADIX, 128), f32),
             pltpu.VMEM((2, 2, GZ, RADIX, 128), f32),
             pltpu.SemaphoreType.DMA((9,)),
-            pltpu.SemaphoreType.DMA((7,)),
-            pltpu.SemaphoreType.DMA((7,)),
+            pltpu.SemaphoreType.DMA((8,)),
+            pltpu.SemaphoreType.DMA((8,)),
             pltpu.SemaphoreType.DMA((8,)),
             pltpu.SemaphoreType.REGULAR((5,)),
         ],

time: 38.2 us -> 37.6 us (0.984)
  Pallas kernels: 36.8 us -> 35.8 us
    pallas_call x1, Pallas kernels: 36.8 us -> 35.8 us  [on_device(): pl.pallas_call(kernel, out_shape=pltpu.VMEM(block, bf16), in_specs=[pl.Bl...]
where the time goes in v8:
time: 37.6 us; the launch traced here: 36.9 us
  Pallas kernels  35.8 us (95%)
  other arithmetic  1.11 us (3%)
    pallas_call x1, Pallas kernels, on_device(): pl.pallas_call(kernel, out_shape=pltpu.VMEM(block, bf16), in_specs=[pl.Bl...  35.8 us
    mul x1, other arithmetic, on_device(): return pressure.astype(f32) * (1.0 / 1024.0)  1.11 us

profile of v8, /device:TPU:1, one launch (start us, length us, event | category | flops | bytes accessed | tf_op | source)
XLA Modules:
  0.0 36.9 jit_solution(9916271915020776479)
XLA Ops:
  0.0 35.8 %poisson.1 = bf16[2,32,32,128]{3,2,1,0:T(8,128)(2,1)S(1)} custom-call(bf16[2,32,32,128]{3,2,1,0:T(8,128)(2,1)} %u_hbm.1, bf16[2,32,32,128]{3,2,1,0:T(8,128)(2,1)} %v_hbm.1, bf16[2,32,32,128]{3,2,1,0:T(8,128)(2,1)} %w_hbm.1, f32[64]{0:T(128)} %spacing_hbm.1, s32[8,128]{1,0:T(8,128)} %bitcast.1, s32[32]{0:T(128)} %plane_hbm.1, ...), custom_call_target="tpu_custom_call" | custom-call | tf_op jit(solution)/shard_map/poisson/pallas_call | solution.py:663
  35.8 1.1 %convert_multiply_fusion = f32[2,32,32,128]{3,2,1,0:T(8,128)} fusion(bf16[2,32,32,128]{3,2,1,0:T(8,128)(2,1)S(1)} %poisson.1), kind=kLoop, calls=%fused_computation | loop fusion | flops 524288 | bytes 1572864 | tf_op jit(solution)/shard_map/mul | solution.py:740

commit v9 on v8

--- a/solution.py
+++ b/solution.py
@@ -352,22 +352,30 @@
 
     columns = [lax.rem(my_x + d, 4) * 2 for d in FAR_FIRST]
 
+    def plane_row(i):
+        return lax.rem(my_y + lax.rem(2 + i + (i // 2) * (1 + 2 * lax.rem(i, 2)), 4), 4) * 8
+
     def sources_for(core, with_sends):
         def source_step(i, carry):
-            base = lax.rem(my_y + lax.rem(2 + i + (i // 2) * (1 + 2 * lax.rem(i, 2)), 4), 4) * 8
+            base = plane_row(i)
             for n in range(4):
                 if with_sends:
                     make_source(base + columns[n] + core)
                 if n > 0:
                     send_s(base + columns[n - 1] + core, core)
-
-            @pl.when(base + columns[3] + core != me)
-            def _():
-                send_s(base + columns[3] + core, core)
+                else:
+
+                    @pl.when(i > 0)
+                    def _():
+                        send_s(plane_row(i - 1) + columns[3] + core, core)
 
             return carry
 
         lax.fori_loop(0, 4, source_step, 0)
+
+        @pl.when(my_core != core)
+        def _():
+            send_s(partner, core)
 
     def s_sent(k, count):
         row_send(s_v.at[:, 0:count], recv_s.at[:, 0:count], k, me).wait_send()

time: 37.6 us -> 37.6 us (level); the launches traced: 36.9 us -> 37.5 us
  Pallas kernels: 35.8 us -> 36.3 us
    pallas_call x1, Pallas kernels: 35.8 us -> 36.3 us  [on_device(): pl.pallas_call(kernel, out_shape=pltpu.VMEM(block, bf16), in_specs=[pl.Bl...]
where the time goes in v9:
time: 37.6 us; the launch traced here: 37.5 us
  Pallas kernels  36.3 us (97%)
  other arithmetic  1.11 us (3%)
    pallas_call x1, Pallas kernels, on_device(): pl.pallas_call(kernel, out_shape=pltpu.VMEM(block, bf16), in_specs=[pl.Bl...  36.3 us
    mul x1, other arithmetic, on_device(): return pressure.astype(f32) * (1.0 / 1024.0)  1.11 us

profile of v9, /device:TPU:1, one launch (start us, length us, event | category | flops | bytes accessed | tf_op | source)
XLA Modules:
  0.0 37.5 jit_solution(16790549377379137399)
XLA Ops:
  0.0 36.3 %poisson.1 = bf16[2,32,32,128]{3,2,1,0:T(8,128)(2,1)S(1)} custom-call(bf16[2,32,32,128]{3,2,1,0:T(8,128)(2,1)} %u_hbm.1, bf16[2,32,32,128]{3,2,1,0:T(8,128)(2,1)} %v_hbm.1, bf16[2,32,32,128]{3,2,1,0:T(8,128)(2,1)} %w_hbm.1, f32[64]{0:T(128)} %spacing_hbm.1, s32[8,128]{1,0:T(8,128)} %bitcast.1, s32[32]{0:T(128)} %plane_hbm.1, ...), custom_call_target="tpu_custom_call" | custom-call | tf_op jit(solution)/shard_map/poisson/pallas_call | solution.py:671
  36.3 1.1 %convert_multiply_fusion = f32[2,32,32,128]{3,2,1,0:T(8,128)} fusion(bf16[2,32,32,128]{3,2,1,0:T(8,128)(2,1)S(1)} %poisson.1), kind=kLoop, calls=%fused_computation | loop fusion | flops 524288 | bytes 1572864 | tf_op jit(solution)/shard_map/mul | solution.py:748
